TPU v7x, 256 devices: a whole 4x4x8 slice. The times are simulated.
256 devices in a mesh: ta: 128 (over y_lo, x, z, core), aa: 2 (over y_hi).
Axes of the slice: x: 4, y: 4 (y_hi: 2, y_lo: 2; y = y_hi * 2 + y_lo), z: 8, core: 2. Of those that a mesh axis runs over, the one named last changes fastest.
Arguments:
- voltages: bfloat16 [256, 3145728], P('aa', 'ta'), may hold values from -6 to 6
- pfb_window: float32 [4, 8192], replicated, may hold values from -3 to 3
Outputs:
- visibilities: float32 [2048, 256, 512], P('ta', 'aa')
All inputs are finite; a program needn't handle non-finite values.
Results may differ from a plain program's by a relative error of at most 0.0026.
Values may be sent and summed in bfloat16 or wider, within the bound.
No kernel may reach another device: no remote copies, remote signals or barrier semaphores. Data moves between devices by JAX's collectives and lax.ppermute only.
A program may use at most 128 MiB of HBM per device.

v0:
```python
import math

import jax
import jax.numpy as jnp
import numpy as np
from jax import lax
from jax.experimental import pallas as pl
from jax.experimental.pallas import tpu as pltpu
from jax.sharding import PartitionSpec as P

NFFT = 8192
CH = 2048
TAPS = 4
CH_OFF = 1024
N1 = 64
N2 = 128
NK = 33
NJ = CH // N1
K2 = CH_OFF // N1
HALF = math.sqrt(0.5)
BF = jnp.bfloat16
F32 = jnp.float32


def twiddle_table():
    phase = np.outer(np.arange(NK), np.arange(N2)) * (2.0 * np.pi / NFFT)
    return np.stack([np.cos(phase), np.sin(phase)], axis=1).astype(np.float32)


def bin_table():
    scale = 1.0 / math.sqrt(NFFT)
    bins = np.arange(K2, K2 + NJ)
    rows = []
    for bin_set, sign in ((bins, 1.0), (-(bins + 1), -1.0)):
        phase = np.outer(bin_set, np.arange(N2)) % N2 * (2.0 * np.pi / N2)
        cosine, sine = np.cos(phase) * scale, np.sin(phase) * scale
        rows.append(np.concatenate([cosine, sine], axis=1))
        rows.append(sign * np.concatenate([-sine, cosine], axis=1))
    table = np.concatenate(rows, axis=0)
    high = table.astype(BF)
    low = (table - high.astype(np.float64)).astype(BF)
    return np.concatenate([high, low], axis=0)


def real_dft8(x):
    s0, d0 = x[0] + x[4], x[0] - x[4]
    s1, d1 = x[1] + x[5], x[1] - x[5]
    s2, d2 = x[2] + x[6], x[2] - x[6]
    s3, d3 = x[3] + x[7], x[3] - x[7]
    e0, e1 = s0 + s2, s1 + s3
    u, v = HALF * (d1 - d3), HALF * (d1 + d3)
    return [(e0 + e1, None), (d0 + u, -(d2 + v)), (s0 - s2, s3 - s1), (d0 - u, d2 - v), (e0 - e1, None)]


def complex_dft8(z, first_half=False):
    sr = [z[j][0] + z[j + 4][0] for j in range(4)]
    si = [z[j][1] + z[j + 4][1] for j in range(4)]
    dr = [z[j][0] - z[j + 4][0] for j in range(4)]
    di = [z[j][1] - z[j + 4][1] for j in range(4)]
    out = [None] * 8
    pr, pi = dr[1], di[1]
    dr[1], di[1] = HALF * (pr + pi), HALF * (pi - pr)
    dr[2], di[2] = di[2], -dr[2]
    pr, pi = dr[3], di[3]
    dr[3], di[3] = HALF * (pi - pr), -HALF * (pr + pi)
    for base, (ar, ai) in ((0, (sr, si)), (1, (dr, di))):
        er, ei = ar[0] + ar[2], ai[0] + ai[2]
        fr, fi = ar[1] + ar[3], ai[1] + ai[3]
        gr, gi = ar[0] - ar[2], ai[0] - ai[2]
        hr, hi = ar[1] - ar[3], ai[1] - ai[3]
        out[base] = (er + fr, ei + fi)
        out[base + 2] = (gr + hi, gi - hr)
        if not first_half:
            out[base + 4] = (er - fr, ei - fi)
            out[base + 6] = (gr - hi, gi + hr)
    return out


def first_half_bins(sections, tw_ref, zhi_ref, zlo_ref, frame, rows):
    def keep(k1, re, im, conj):
        c, s = tw_ref[k1, 0:1, :], tw_ref[k1, 1:2, :]
        if im is None:
            zr, zi = re * c, -(re * s)
        elif conj:
            zr, zi = re * c - im * s, -(im * c + re * s)
        else:
            zr, zi = re * c + im * s, im * c - re * s
        for part, z in ((0, zr), (1, zi)):
            high = z.astype(BF)
            low = (z - high.astype(F32)).astype(BF)
            zhi_ref[k1, rows, part * N2 : (part + 1) * N2] = high
            zlo_ref[k1, rows, part * N2 : (part + 1) * N2] = low

    spectrum = real_dft8([sections[frame, 0, b] for b in range(8)])
    for r in range(5):
        keep(8 * r, spectrum[r][0], spectrum[r][1], False)
    for q in (1, 2, 3):
        z = []
        for b in range(8):
            re, im = sections[frame, 2 * q - 1, b], sections[frame, 2 * q, b]
            if b:
                c, s = math.cos(2 * math.pi * b * q / N1), math.sin(2 * math.pi * b * q / N1)
                re, im = re * c + im * s, im * c - re * s
            z.append((re, im))
        for r, (re, im) in enumerate(complex_dft8(z)):
            k1 = q + 8 * r
            if k1 <= 32:
                keep(k1, re, im, False)
            else:
                keep(N1 - k1, re, im, True)
    z = []
    for b in range(8):
        x = sections[frame, 7, b]
        c, s = math.cos(2 * math.pi * b * 4 / N1), math.sin(2 * math.pi * b * 4 / N1)
        z.append((x * c, x * -s) if b else (x, jnp.zeros_like(x)))
    out = complex_dft8(z, first_half=True)
    for r in range(4):
        keep(4 + 8 * r, out[r][0], out[r][1], False)


def sections_of(frames_of, n_out, w_ref, sections):
    for b in range(8):
        filtered = [[] for _ in range(n_out)]
        for a in range(8):
            n1 = 8 * a + b
            w = [w_ref[k : k + 1, n1 * N2 : (n1 + 1) * N2] for k in range(TAPS)]
            for f, value in enumerate(frames_of(n1, w)):
                filtered[f].append(value)
        for f in range(n_out):
            spectrum = real_dft8(filtered[f])
            sections[f, 0, b] = spectrum[0][0]
            for q in (1, 2, 3):
                sections[f, 2 * q - 1, b] = spectrum[q][0]
                sections[f, 2 * q, b] = spectrum[q][1]
            sections[f, 7, b] = spectrum[4][0]


def frame_at(ref, frame, n1):
    at = frame * NFFT + n1 * N2
    return ref[:, at : at + N2].astype(F32)


def emit_slabs(n_out, table_ref, zhi_ref, zlo_ref, wide_ref, out_ref):
    slab = n_out * 16

    def one(k1, mirror):
        dims = (((1,), (1,)), ((), ()))
        both = lax.dot_general(table_ref[...], zhi_ref[k1], dims, preferred_element_type=F32)
        more = lax.dot_general(table_ref[0:N2, :], zlo_ref[k1], dims, preferred_element_type=F32)
        spectrum = both[:N2] + both[N2:] + more
        for side in range(2 if mirror else 1):
            ch = N1 - k1 if side else k1
            start = (ch // 8) * slab + ch % 8
            for part in range(2):
                at = (side * 2 + part) * NJ
                for f in range(n_out):
                    wide_ref[pl.ds(start + (f * 2 + part) * 8, NJ, stride=8 * slab), :] = spectrum[
                        at : at + NJ, f * N2 : (f + 1) * N2
                    ]

    one(0, False)

    def body(k1, carry):
        one(k1, True)
        return carry

    lax.fori_loop(1, NK, body, 0)

    def narrow(p, carry):
        at = pl.multiple_of(p * (4 * slab), 4 * slab)
        out_ref[pl.ds(at, 4 * slab), :] = wide_ref[pl.ds(at, 4 * slab), :].astype(BF)
        return carry

    lax.fori_loop(0, CH // 32, narrow, 0)


def pair_kernel(mask_ref, prev_ref, v_ref, next_ref, w_ref, tw_ref, table_ref, out_ref, sections, zhi, zlo, wide):
    group = pl.program_id(0)
    keep = mask_ref[0].astype(F32)

    def frames_of(n1, w):
        p2, v0, v1, v2, n0 = (
            frame_at(prev_ref, 0, n1),
            frame_at(v_ref, 0, n1),
            frame_at(v_ref, 1, n1),
            frame_at(v_ref, 2, n1),
            frame_at(next_ref, 0, n1),
        )
        return (
            w[0] * p2 + w[1] * v0 + w[2] * v1 + w[3] * v2,
            keep * (w[0] * v0 + w[1] * v1 + w[2] * v2) + w[3] * n0,
        )

    sections_of(frames_of, 2, w_ref, sections)
    for f in range(2):
        rows = pl.ds(pl.multiple_of(f * N2 + group * 16, 16), 16)
        first_half_bins(sections, tw_ref, zhi, zlo, f, rows)

    @pl.when(group == pl.num_programs(0) - 1)
    def _():
        emit_slabs(2, table_ref, zhi, zlo, wide, out_ref)


def single_kernel(
    mask_ref, prev_ref, v_ref, next_ref, side_ref, w_ref, tw_ref, table_ref, out_ref, sections, zhi, zlo, wide
):
    group = pl.program_id(0)
    keep = mask_ref[0].astype(F32)
    half = pl.num_programs(0) // 2

    @pl.when(group < half)
    def _():
        def frames_of(n1, w):
            return (
                w[0] * frame_at(side_ref, 0, n1)
                + w[1] * frame_at(prev_ref, 0, n1)
                + w[2] * frame_at(v_ref, 0, n1)
                + w[3] * frame_at(v_ref, 1, n1),
            )

        sections_of(frames_of, 1, w_ref, sections)

    @pl.when(group >= half)
    def _():
        def frames_of(n1, w):
            return (
                keep * (w[0] * frame_at(v_ref, 1, n1) + w[1] * frame_at(v_ref, 2, n1))
                + w[2] * frame_at(next_ref, 0, n1)
                + w[3] * frame_at(side_ref, 0, n1),
            )

        sections_of(frames_of, 1, w_ref, sections)

    first_half_bins(sections, tw_ref, zhi, zlo, 0, pl.ds(pl.multiple_of(group * 16, 16), 16))

    @pl.when(group == pl.num_programs(0) - 1)
    def _():
        emit_slabs(1, table_ref, zhi, zlo, wide, out_ref)


def spectra_call(body, n_out, mask, signal_arrays, window):
    signals = signal_arrays[0].shape[0]
    groups = signals // 16
    by_group = [pl.BlockSpec((16, x.shape[1]), lambda g: (g, 0)) for x in signal_arrays]
    whole = lambda shape: pl.BlockSpec(shape, lambda g: (0,) * len(shape))
    rows = CH * 2 * n_out
    return pl.pallas_call(
        body,
        out_shape=jax.ShapeDtypeStruct((rows, N2), BF),
        grid=(groups,),
        in_specs=[
            pl.BlockSpec(memory_space=pltpu.SMEM),
            *by_group,
            whole((TAPS, NFFT)),
            whole((NK, 2, N2)),
            whole((2 * N2, 2 * N2)),
        ],
        out_specs=whole((rows, N2)),
        scratch_shapes=[
            pltpu.VMEM((n_out, 8, 8, 16, N2), F32),
            pltpu.VMEM((NK, n_out * N2, 2 * N2), BF),
            pltpu.VMEM((NK, n_out * N2, 2 * N2), BF),
            pltpu.VMEM((rows, N2), F32),
        ],
        cost_estimate=pl.CostEstimate(flops=n_out * 10**10, transcendentals=0, bytes_accessed=n_out * 10**7),
        compiler_params=pltpu.CompilerParams(
            dimension_semantics=("arbitrary",), vmem_limit_bytes=56 * 1024 * 1024
        ),
    )(mask, *signal_arrays, window, jnp.asarray(twiddle_table()), jnp.asarray(bin_table()))


def correlate_kernel(own_ref, pair_ref, single_ref, out_ref, send_ref, wide, real, imag):
    ch = pl.program_id(0)
    own = own_ref[0]
    frames = 3 * N2
    scale = 1.0 / math.sqrt(frames)

    @pl.when(ch == 0)
    def _():
        first_lanes = lax.broadcasted_iota(jnp.int32, (16, N2), 1) < N2 // 2

        def body(t, carry):
            for src in range(2):
                for f in range(3):
                    ref, per, skip = (pair_ref, 32, f * 16) if f < 2 else (single_ref, 16, 0)
                    row = pl.multiple_of((t * 2 + src) * per + skip, 16)
                    tile = ref[pl.ds(row, 16), :].astype(F32)
                    if f == 2:
                        row = pl.multiple_of(((t + N2 - 1) % N2 * 2 + src) * per, 16)
                        tile = jnp.where(first_lanes, tile, ref[pl.ds(row, 16), :].astype(F32))
                    for part in range(2):
                        at = part * frames + f * N2 + t
                        wide[src, pl.ds(at, 8, stride=2 * frames), :] = tile[part * 8 : part * 8 + 8]
            return carry

        lax.fori_loop(0, N2, body, 0)

    at = pl.multiple_of(ch * 2 * frames, 2 * frames)
    rows = pl.ds(at, 2 * frames)
    both = jnp.concatenate([wide[0, rows, :].astype(BF), wide[1, rows, :].astype(BF)], axis=1)
    xr, xi = both[:frames], both[frames:]
    dims = (((0,), (0,)), ((), ()))
    r = lax.dot_general(both, both, dims, preferred_element_type=F32) * scale
    p = lax.dot_general(xi, xr, dims, preferred_element_type=F32) * scale
    real[...] = r
    imag[...] = p - p.T
    mine = pl.ds(pl.multiple_of(own * N2, N2), N2)
    theirs = pl.ds(pl.multiple_of((1 - own) * N2, N2), N2)
    out_ref[0, :, : 2 * N2] = real[mine, :]
    out_ref[0, :, 2 * N2 :] = imag[mine, :]
    rows_r, rows_i = real[theirs, :], imag[theirs, :]
    first = own == 0
    cross_r = jnp.where(first, rows_r[:, :N2], rows_r[:, N2:])
    cross_i = jnp.where(first, rows_i[:, :N2], rows_i[:, N2:])
    diag_r = jnp.where(first, rows_r[:, N2:], rows_r[:, :N2])
    diag_i = jnp.where(first, rows_i[:, N2:], rows_i[:, :N2])
    upper = lax.broadcasted_iota(jnp.int32, (N2, N2), 0) <= lax.broadcasted_iota(jnp.int32, (N2, N2), 1)
    send_ref[0, :, :N2] = cross_r.astype(BF)
    send_ref[0, :, N2 : 2 * N2] = cross_i.astype(BF)
    send_ref[0, :, 2 * N2 :] = jnp.where(upper, diag_r, diag_i).astype(BF)


def correlate(own, pair, single):
    frames = 3 * N2
    grid_spec = pltpu.PrefetchScalarGridSpec(
        num_scalar_prefetch=1,
        grid=(8,),
        in_specs=[
            pl.BlockSpec(pair.shape, lambda c, own: (0, 0)),
            pl.BlockSpec(single.shape, lambda c, own: (0, 0)),
        ],
        out_specs=[
            pl.BlockSpec((1, N2, 4 * N2), lambda c, own: (own[0] * 8 + c, 0, 0)),
            pl.BlockSpec((1, N2, 3 * N2), lambda c, own: (c, 0, 0)),
        ],
        scratch_shapes=[
            pltpu.VMEM((2, 8 * 2 * frames, N2), F32),
            pltpu.VMEM((2 * N2, 2 * N2), F32),
            pltpu.VMEM((2 * N2, 2 * N2), F32),
        ],
    )
    return pl.pallas_call(
        correlate_kernel,
        out_shape=[
            jax.ShapeDtypeStruct((16, N2, 4 * N2), F32),
            jax.ShapeDtypeStruct((8, N2, 3 * N2), BF),
        ],
        grid_spec=grid_spec,
        cost_estimate=pl.CostEstimate(flops=10**10, transcendentals=0, bytes_accessed=10**7),
        compiler_params=pltpu.CompilerParams(
            dimension_semantics=("arbitrary",), vmem_limit_bytes=40 * 1024 * 1024
        ),
    )(own, pair, single)


def finish_kernel(own_ref, part_ref, got_ref, out_ref):
    first = own_ref[0] == 0
    cross_r = got_ref[0, :, :N2].astype(F32)
    cross_i = got_ref[0, :, N2 : 2 * N2].astype(F32)
    packed = got_ref[0, :, 2 * N2 :].astype(F32)
    flipped = packed.T
    row = lax.broadcasted_iota(jnp.int32, (N2, N2), 0)
    col = lax.broadcasted_iota(jnp.int32, (N2, N2), 1)
    diag_r = jnp.where(row <= col, packed, flipped)
    diag_i = jnp.where(row > col, packed, jnp.where(row < col, -flipped, 0.0))
    out_ref[0, :, :N2] = jnp.where(first, diag_r, cross_r)
    out_ref[0, :, N2 : 2 * N2] = jnp.where(first, cross_r, diag_r)
    out_ref[0, :, 2 * N2 : 3 * N2] = jnp.where(first, diag_i, cross_i)
    out_ref[0, :, 3 * N2 :] = jnp.where(first, cross_i, diag_i)


def finish(own, part, got):
    grid_spec = pltpu.PrefetchScalarGridSpec(
        num_scalar_prefetch=1,
        grid=(8,),
        in_specs=[
            pl.BlockSpec(memory_space=pl.ANY),
            pl.BlockSpec((1, N2, 3 * N2), lambda c, own: (c, 0, 0)),
        ],
        out_specs=pl.BlockSpec((1, N2, 4 * N2), lambda c, own: ((1 - own[0]) * 8 + c, 0, 0)),
    )
    return pl.pallas_call(
        finish_kernel,
        out_shape=jax.ShapeDtypeStruct(part.shape, F32),
        grid_spec=grid_spec,
        input_output_aliases={1: 0},
        compiler_params=pltpu.CompilerParams(dimension_semantics=("arbitrary",)),
    )(own, part, got)


def per_device(voltages, pfb_window):
    signals = voltages.shape[0]
    peers = lax.axis_size("ta")
    half = signals // 2
    to_right = [(i, i + 1) for i in range(peers - 1)]
    to_left = [(i, (i - 1) % peers) for i in range(peers)]
    inner = (lax.axis_index("ta") < peers - 1).astype(jnp.int32).reshape(1)
    own = lax.axis_index("aa").astype(jnp.int32).reshape(1)
    prev = lax.ppermute(voltages[:, 2 * NFFT :], "ta", to_right)
    following = lax.ppermute(voltages[:, :NFFT], "ta", to_left)
    prev_side = lax.ppermute(voltages[:half, NFFT : 2 * NFFT], "ta", to_right)
    next_side = lax.ppermute(voltages[half:, NFFT : 2 * NFFT], "ta", to_left)
    pair = spectra_call(pair_kernel, 2, inner, (prev, voltages, following), pfb_window)
    pair = lax.all_to_all(pair, ("ta", "aa"), split_axis=0, concat_axis=0, tiled=True)
    side = jnp.concatenate([prev_side, next_side], axis=0)
    single = spectra_call(single_kernel, 1, inner, (prev, voltages, following, side), pfb_window)
    single = lax.all_to_all(single, ("ta", "aa"), split_axis=0, concat_axis=0, tiled=True)
    part, send = correlate(own, pair, single)
    got = lax.ppermute(send, "aa", [(0, 1), (1, 0)])
    return finish(own, part, got)


def solution(mesh):
    return jax.shard_map(
        per_device,
        mesh=mesh,
        in_specs=(P("aa", "ta"), P()),
        out_specs=P("ta", "aa", None),
        check_vma=False,
    )
```

profile of v0, /device:TPU:64, one launch (start us, length us, event | category | flops | bytes accessed | tf_op | source)
XLA Modules:
  0.0 207.9 jit_solution(18264011027666891531)
XLA Ops:
  0.0 3.9 %fusion.1 = (bf16[128,8192]{1,0:T(8,128)(2,1)}, bf16[128,8192]{1,0:T(8,128)(2,1)S(1)}) fusion(bf16[128,24576]{1,0:T(8,128)(2,1)} %v_ref.3), kind=kLoop, calls=%fused_computation.2 | loop fusion | bytes 8388608 | tf_op jit(solution)/shard_map/slice | solution.py:400
  3.9 0.0 collective-permute-start.1
  3.9 2.4 %collective-permute-start = (bf16[128,8192]{1,0:T(8,128)(2,1)S(1)}, bf16[128,8192]{1,0:T(8,128)(2,1)}, u32[]{:S(2)}, u32[]{:S(2)}) collective-permute-start(bf16[128,8192]{1,0:T(8,128)(2,1)S(1)} %get-tuple-element.12), channel_id=1, source_target_pairs={{0,2},{2,4},{4,6},{6,8},{8,10},{10,12},{12,14},{14,16},{16,18},{18... | collective-permute-start | bytes 6291464 | tf_op jit(solution)/shard_map/ppermute | solution.py:399
  6.3 3.0 %fusion = (bf16[64,8192]{1,0:T(8,128)(2,1)}, bf16[64,8192]{1,0:T(8,128)(2,1)}) fusion(bf16[128,24576]{1,0:T(8,128)(2,1)} %v_ref.3), kind=kLoop, calls=%fused_computation.1 | loop fusion | bytes 4194304 | tf_op jit(solution)/shard_map/slice | solution.py:401
  9.4 3.4 %collective-permute-start.2 = (bf16[64,8192]{1,0:T(8,128)(2,1)}, bf16[64,8192]{1,0:T(8,128)(2,1)S(1)}, u32[]{:S(2)}, u32[]{:S(2)}) collective-permute-start(bf16[64,8192]{1,0:T(8,128)(2,1)} %get-tuple-element.9), channel_id=1, source_target_pairs={{0,2},{2,4},{4,6},{6,8},{8,10},{10,12},{12,14},{14,16},{16,18},{18... | collective-permute-start | bytes 3145736 | tf_op jit(solution)/shard_map/ppermute | solution.py:401
  12.8 0.3 collective-permute-start.3
  13.1 29.4 %collective-permute-done.2 = bf16[64,8192]{1,0:T(8,128)(2,1)S(1)} collective-permute-done((bf16[64,8192]{1,0:T(8,128)(2,1)}, bf16[64,8192]{1,0:T(8,128)(2,1)S(1)}, u32[]{:S(2)}, u32[]{:S(2)}) %collective-permute-start.2) | collective-permute-done | bytes 1048608 | tf_op jit(solution)/shard_map/ppermute | solution.py:401
  42.5 0.0 collective-permute-done.3
  42.5 2.7 %pad_maximum_fusion.side_ref = bf16[128,8192]{1,0:T(8,128)(2,1)} fusion(bf16[64,8192]{1,0:T(8,128)(2,1)} %collective-permute-done.3, bf16[64,8192]{1,0:T(8,128)(2,1)S(1)} %collective-permute-done.2), kind=kLoop, calls=%fused_computation | loop fusion | flops 4194304 | bytes 4194304 | tf_op jit(solution)/shard_map/concatenate | solution.py:405
  45.2 0.0 collective-permute-done.1.next_ref
  45.2 0.0 collective-permute-done.prev_ref
  45.2 18.8 %shard_map.65 = bf16[4096,128]{1,0:T(8,128)(2,1)} custom-call(s32[1]{0:T(128)} %bitcast.1.mask_ref, bf16[128,8192]{1,0:T(8,128)(2,1)} %collective-permute-done.prev_ref, bf16[128,24576]{1,0:T(8,128)(2,1)} %v_ref.3, bf16[128,8192]{1,0:T(8,128)(2,1)} %collective-permute-done.1.next_ref, bf16[128,8192]{1,0:T(8,128)(2,1)} %pad_maximum_fusion.side_ref, ...), custom_call_target="tpu_custom_call" | custom-call | flops 10000000000 | bytes 10000000 | tf_op jit(solution)/shard_map/pallas_call | solution.py:247
  64.0 16.8 %all-to-all-start.1 = ((bf16[256,16,128]{2,1,0:T(8,128)(2,1)}), bf16[256,16,128]{2,1,0:T(8,128)(2,1)S(1)}, u32[]{:S(2)}, u32[]{:S(2)}) async-start(bf16[256,16,128]{2,1,0:T(8,128)(2,1)} %bitcast.9), calls=%async_computation.1 | async-start | bytes 2097152 | tf_op jit(solution)/shard_map/all_to_all | solution.py:407
  80.8 22.9 %shard_map.64 = bf16[8192,128]{1,0:T(8,128)(2,1)} custom-call(s32[1]{0:T(128)} %bitcast.1.mask_ref, bf16[128,8192]{1,0:T(8,128)(2,1)} %collective-permute-done.prev_ref, bf16[128,24576]{1,0:T(8,128)(2,1)} %v_ref.3, bf16[128,8192]{1,0:T(8,128)(2,1)} %collective-permute-done.1.next_ref, f32[4,8192]{1,0:T(4,128)} %w_ref.3, ...), custom_call_target="tpu_custom_call" | custom-call | flops 20000000000 | bytes 20000000 | tf_op jit(solution)/shard_map/pallas_call | solution.py:247
  103.8 5.9 %all-to-all-done.1 = bf16[256,16,128]{2,1,0:T(8,128)(2,1)S(1)} async-done(((bf16[256,16,128]{2,1,0:T(8,128)(2,1)}), bf16[256,16,128]{2,1,0:T(8,128)(2,1)S(1)}, u32[]{:S(2)}, u32[]{:S(2)}) %all-to-all-start.1) | async-done | bytes 1048608 | tf_op jit(solution)/shard_map/all_to_all | solution.py:407
  109.6 8.1 %all-to-all-start = ((bf16[256,32,128]{2,1,0:T(8,128)(2,1)}), bf16[256,32,128]{2,1,0:T(8,128)(2,1)S(1)}, u32[]{:S(2)}, u32[]{:S(2)}) async-start(bf16[256,32,128]{2,1,0:T(8,128)(2,1)} %bitcast.8), calls=%async_computation | async-start | bytes 4194304 | tf_op jit(solution)/shard_map/all_to_all | solution.py:404
  117.8 50.6 %all-to-all-done = bf16[256,32,128]{2,1,0:T(8,128)(2,1)S(1)} async-done(((bf16[256,32,128]{2,1,0:T(8,128)(2,1)}), bf16[256,32,128]{2,1,0:T(8,128)(2,1)S(1)}, u32[]{:S(2)}, u32[]{:S(2)}) %all-to-all-start) | async-done | bytes 2097184 | tf_op jit(solution)/shard_map/all_to_all | solution.py:404
  168.4 11.9 %shard_map.66 = (f32[16,128,512]{2,1,0:T(8,128)}, bf16[8,128,384]{2,1,0:T(8,128)(2,1)S(1)}) custom-call(s32[1]{0:T(128)} %bitcast.own_ref, bf16[8192,128]{1,0:T(8,128)(2,1)S(1)} %bitcast.6, bf16[4096,128]{1,0:T(8,128)(2,1)S(1)} %bitcast.7), custom_call_target="tpu_custom_call" | custom-call | flops 10000000000 | bytes 10000000 | tf_op jit(solution)/shard_map/pallas_call | solution.py:342
  180.3 1.6 collective-permute-start.4
  181.9 19.4 %collective-permute-done.4.got_ref = bf16[8,128,384]{2,1,0:T(8,128)(2,1)S(1)} collective-permute-done((bf16[8,128,384]{2,1,0:T(8,128)(2,1)S(1)}, bf16[8,128,384]{2,1,0:T(8,128)(2,1)S(1)}, u32[]{:S(2)}, u32[]{:S(2)}) %collective-permute-start.4) | collective-permute-done | bytes 786464 | tf_op jit(solution)/shard_map/ppermute | solution.py:409
  201.3 0.0 copy-start
  201.3 0.9 copy-done
  202.2 5.6 %shard_map.67 = f32[16,128,512]{2,1,0:T(8,128)} custom-call(s32[1]{0:T(128)} %bitcast.own_ref, f32[16,128,512]{2,1,0:T(8,128)} %get-tuple-element.7.part_ref, bf16[8,128,384]{2,1,0:T(8,128)(2,1)} %copy-done), custom_call_target="tpu_custom_call", output_to_operand_aliasing={{}: (1, {})} | custom-call | tf_op jit(solution)/shard_map/pallas_call | solution.py:382
Async XLA Ops:
  3.9 41.3 %collective-permute-start.1 = (bf16[128,8192]{1,0:T(8,128)(2,1)}, bf16[128,8192]{1,0:T(8,128)(2,1)}, u32[]{:S(2)}, u32[]{:S(2)}) collective-permute-start(bf16[128,8192]{1,0:T(8,128)(2,1)} %get-tuple-element.11), channel_id=1, source_target_pairs={{0,254},{2,0},{4,2},{6,4},{8,6},{10,8},{12,10},{14,12},{16,14},{18... | collective-permute-start | bytes 6291464 | tf_op jit(solution)/shard_map/ppermute | solution.py:400
  3.9 41.3 %collective-permute-start = (bf16[128,8192]{1,0:T(8,128)(2,1)S(1)}, bf16[128,8192]{1,0:T(8,128)(2,1)}, u32[]{:S(2)}, u32[]{:S(2)}) collective-permute-start(bf16[128,8192]{1,0:T(8,128)(2,1)S(1)} %get-tuple-element.12), channel_id=1, source_target_pairs={{0,2},{2,4},{4,6},{6,8},{8,10},{10,12},{12,14},{14,16},{16,18},{18... | collective-permute-start | bytes 6291464 | tf_op jit(solution)/shard_map/ppermute | solution.py:399
  9.4 33.1 %collective-permute-start.2 = (bf16[64,8192]{1,0:T(8,128)(2,1)}, bf16[64,8192]{1,0:T(8,128)(2,1)S(1)}, u32[]{:S(2)}, u32[]{:S(2)}) collective-permute-start(bf16[64,8192]{1,0:T(8,128)(2,1)} %get-tuple-element.9), channel_id=1, source_target_pairs={{0,2},{2,4},{4,6},{6,8},{8,10},{10,12},{12,14},{14,16},{16,18},{18... | collective-permute-start | bytes 3145736 | tf_op jit(solution)/shard_map/ppermute | solution.py:401
  12.8 29.7 %collective-permute-start.3 = (bf16[64,8192]{1,0:T(8,128)(2,1)}, bf16[64,8192]{1,0:T(8,128)(2,1)}, u32[]{:S(2)}, u32[]{:S(2)}) collective-permute-start(bf16[64,8192]{1,0:T(8,128)(2,1)} %get-tuple-element.10), channel_id=1, source_target_pairs={{0,254},{2,0},{4,2},{6,4},{8,6},{10,8},{12,10},{14,12},{16,14},{18... | collective-permute-start | bytes 3145736 | tf_op jit(solution)/shard_map/ppermute | solution.py:402
  64.0 45.6 %all-to-all-start.1 = ((bf16[256,16,128]{2,1,0:T(8,128)(2,1)}), bf16[256,16,128]{2,1,0:T(8,128)(2,1)S(1)}, u32[]{:S(2)}, u32[]{:S(2)}) async-start(bf16[256,16,128]{2,1,0:T(8,128)(2,1)} %bitcast.9), calls=%async_computation.1 | async-start | bytes 2097152 | tf_op jit(solution)/shard_map/all_to_all | solution.py:407
  109.6 58.7 %all-to-all-start = ((bf16[256,32,128]{2,1,0:T(8,128)(2,1)}), bf16[256,32,128]{2,1,0:T(8,128)(2,1)S(1)}, u32[]{:S(2)}, u32[]{:S(2)}) async-start(bf16[256,32,128]{2,1,0:T(8,128)(2,1)} %bitcast.8), calls=%async_computation | async-start | bytes 4194304 | tf_op jit(solution)/shard_map/all_to_all | solution.py:404
  180.3 21.1 %collective-permute-start.4 = (bf16[8,128,384]{2,1,0:T(8,128)(2,1)S(1)}, bf16[8,128,384]{2,1,0:T(8,128)(2,1)S(1)}, u32[]{:S(2)}, u32[]{:S(2)}) collective-permute-start(bf16[8,128,384]{2,1,0:T(8,128)(2,1)S(1)} %get-tuple-element.8), channel_id=1, source_target_pairs={{0,1},{1,0},{2,3},{3,2},{4,5},{5,4},{6,7},{7,6},{8,9},{9,8},{10,11... | collective-permute-start | bytes 2359304 | tf_op jit(solution)/shard_map/ppermute | solution.py:409
  201.3 0.9 copy-start
where the time goes:
time: 211 us; the launch traced here: 208 us
  waiting for transfers between devices  105 us (50%)
  Pallas kernels  59.3 us (28%)
  starting transfers between devices  32.7 us (15%)
  local copies, waits for them, and re-layouts  7.84 us (4%)
  other arithmetic  2.73 us (1%)
    all_to_all x1, waiting for transfers between devices, per_device(): lax.all_to_all(pair, ('ta', 'aa'), split_axis=0, concat_axis=0, tiled=True)  50.6 us
    pallas_call x2, Pallas kernels, spectra_call(): pl.pallas_call(body, out_shape=jax.ShapeDtypeStruct((rows, N2), BF), grid...  41.7 us
    ppermute x1, waiting for transfers between devices, per_device(): prev_side = lax.ppermute(voltages[:half, NFFT:2 * NFFT], 'ta', to_right)  29.4 us
    ppermute x1, waiting for transfers between devices, per_device(): got = lax.ppermute(send, 'aa', [(0, 1), (1, 0)])  19.4 us
    all_to_all x1, starting transfers between devices, per_device(): lax.all_to_all(single, ('ta', 'aa'), split_axis=0, concat_axis=0, tiled=T...  16.8 us
    pallas_call x1, Pallas kernels, correlate(): pl.pallas_call(correlate_kernel, out_shape=[jax.ShapeDtypeStruct((16, N2,...  11.9 us
    all_to_all x1, starting transfers between devices, per_device(): lax.all_to_all(pair, ('ta', 'aa'), split_axis=0, concat_axis=0, tiled=True)  8.14 us
    all_to_all x1, waiting for transfers between devices, per_device(): lax.all_to_all(single, ('ta', 'aa'), split_axis=0, concat_axis=0, tiled=T...  5.88 us
  transfers between devices with their start and end apart: 7, of which 4 were waited for; matrix products, arithmetic and copies ran while one was open for 3% of the time, Pallas kernels for 11%

commit v1 on v0

v1 whole, which is shorter than its diff:
```python
import math

import jax
import jax.numpy as jnp
import numpy as np
from jax import lax
from jax.experimental import pallas as pl
from jax.experimental.pallas import tpu as pltpu
from jax.sharding import PartitionSpec as P

NFFT = 8192
CH = 2048
TAPS = 4
CH_OFF = 1024
N1 = 64
N2 = 128
NK = 33
NJ = CH // N1
K2 = CH_OFF // N1
HALF = math.sqrt(0.5)
BF = jnp.bfloat16
F32 = jnp.float32


def twiddle_table():
    phase = np.outer(np.arange(NK), np.arange(N2)) * (2.0 * np.pi / NFFT)
    return np.stack([np.cos(phase), np.sin(phase)], axis=1).astype(np.float32)


def bin_table():
    scale = 1.0 / math.sqrt(NFFT)
    bins = np.arange(K2, K2 + NJ)
    rows = []
    for bin_set, sign in ((bins, 1.0), (-(bins + 1), -1.0)):
        phase = np.outer(bin_set, np.arange(N2)) % N2 * (2.0 * np.pi / N2)
        cosine, sine = np.cos(phase) * scale, np.sin(phase) * scale
        rows.append(np.concatenate([cosine, sine], axis=1))
        rows.append(sign * np.concatenate([-sine, cosine], axis=1))
    table = np.concatenate(rows, axis=0)
    high = table.astype(BF)
    low = (table - high.astype(np.float64)).astype(BF)
    return np.concatenate([high, low], axis=0)


def real_dft8(x):
    s0, d0 = x[0] + x[4], x[0] - x[4]
    s1, d1 = x[1] + x[5], x[1] - x[5]
    s2, d2 = x[2] + x[6], x[2] - x[6]
    s3, d3 = x[3] + x[7], x[3] - x[7]
    e0, e1 = s0 + s2, s1 + s3
    u, v = HALF * (d1 - d3), HALF * (d1 + d3)
    return [(e0 + e1, None), (d0 + u, -(d2 + v)), (s0 - s2, s3 - s1), (d0 - u, d2 - v), (e0 - e1, None)]


def complex_dft8(z, first_half=False):
    sr = [z[j][0] + z[j + 4][0] for j in range(4)]
    si = [z[j][1] + z[j + 4][1] for j in range(4)]
    dr = [z[j][0] - z[j + 4][0] for j in range(4)]
    di = [z[j][1] - z[j + 4][1] for j in range(4)]
    out = [None] * 8
    pr, pi = dr[1], di[1]
    dr[1], di[1] = HALF * (pr + pi), HALF * (pi - pr)
    dr[2], di[2] = di[2], -dr[2]
    pr, pi = dr[3], di[3]
    dr[3], di[3] = HALF * (pi - pr), -HALF * (pr + pi)
    for base, (ar, ai) in ((0, (sr, si)), (1, (dr, di))):
        er, ei = ar[0] + ar[2], ai[0] + ai[2]
        fr, fi = ar[1] + ar[3], ai[1] + ai[3]
        gr, gi = ar[0] - ar[2], ai[0] - ai[2]
        hr, hi = ar[1] - ar[3], ai[1] - ai[3]
        out[base] = (er + fr, ei + fi)
        out[base + 2] = (gr + hi, gi - hr)
        if not first_half:
            out[base + 4] = (er - fr, ei - fi)
            out[base + 6] = (gr - hi, gi + hr)
    return out


def first_half_bins(sections, tw_ref, zhi_ref, zlo_ref, frame, rows):
    def keep(k1, re, im, conj):
        c, s = tw_ref[k1, 0:1, :], tw_ref[k1, 1:2, :]
        if im is None:
            zr, zi = re * c, -(re * s)
        elif conj:
            zr, zi = re * c - im * s, -(im * c + re * s)
        else:
            zr, zi = re * c + im * s, im * c - re * s
        for part, z in ((0, zr), (1, zi)):
            high = z.astype(BF)
            low = (z - high.astype(F32)).astype(BF)
            zhi_ref[k1, rows, part * N2 : (part + 1) * N2] = high
            zlo_ref[k1, rows, part * N2 : (part + 1) * N2] = low

    spectrum = real_dft8([sections[frame, 0, b] for b in range(8)])
    for r in range(5):
        keep(8 * r, spectrum[r][0], spectrum[r][1], False)
    for q in (1, 2, 3):
        z = []
        for b in range(8):
            re, im = sections[frame, 2 * q - 1, b], sections[frame, 2 * q, b]
            if b:
                c, s = math.cos(2 * math.pi * b * q / N1), math.sin(2 * math.pi * b * q / N1)
                re, im = re * c + im * s, im * c - re * s
            z.append((re, im))
        for r, (re, im) in enumerate(complex_dft8(z)):
            k1 = q + 8 * r
            if k1 <= 32:
                keep(k1, re, im, False)
            else:
                keep(N1 - k1, re, im, True)
    z = []
    for b in range(8):
        x = sections[frame, 7, b]
        c, s = math.cos(2 * math.pi * b * 4 / N1), math.sin(2 * math.pi * b * 4 / N1)
        z.append((x * c, x * -s) if b else (x, jnp.zeros_like(x)))
    out = complex_dft8(z, first_half=True)
    for r in range(4):
        keep(4 + 8 * r, out[r][0], out[r][1], False)


def sections_of(frames_of, n_out, w_ref, sections):
    for b in range(8):
        filtered = [[] for _ in range(n_out)]
        for a in range(8):
            n1 = 8 * a + b
            w = [w_ref[k : k + 1, n1 * N2 : (n1 + 1) * N2] for k in range(TAPS)]
            for f, value in enumerate(frames_of(n1, w)):
                filtered[f].append(value)
        for f in range(n_out):
            spectrum = real_dft8(filtered[f])
            sections[f, 0, b] = spectrum[0][0]
            for q in (1, 2, 3):
                sections[f, 2 * q - 1, b] = spectrum[q][0]
                sections[f, 2 * q, b] = spectrum[q][1]
            sections[f, 7, b] = spectrum[4][0]


def emit_slabs(n_out, table_ref, zhi_ref, zlo_ref, wide_ref, slabs_ref, out_ref, out_sems):
    slab = n_out * 16
    block = 8 * slab
    lap = block + 1

    def one(k1, mirror):
        dims = (((1,), (1,)), ((), ()))
        both = lax.dot_general(table_ref[...], zhi_ref[k1], dims, preferred_element_type=F32)
        more = lax.dot_general(table_ref[0:N2, :], zlo_ref[k1], dims, preferred_element_type=F32)
        spectrum = both[:N2] + both[N2:] + more
        for side in range(2 if mirror else 1):
            ch = N1 - k1 if side else k1
            start = (ch // 8) * slab + ch % 8
            for part in range(2):
                at = (side * 2 + part) * NJ
                for f in range(n_out):
                    wide_ref[pl.ds(start + (f * 2 + part) * 8, NJ, stride=lap), :] = spectrum[
                        at : at + NJ, f * N2 : (f + 1) * N2
                    ]

    one(0, False)

    def body(k1, carry):
        one(k1, True)
        return carry

    lax.fori_loop(1, NK, body, 0)

    def copy_out(j):
        rows = pl.ds(pl.multiple_of(j * block, block), block)
        return pltpu.make_async_copy(slabs_ref.at[rows], out_ref.at[rows], out_sems.at[j])

    def narrow(j, carry):
        slabs_ref[pl.ds(pl.multiple_of(j * block, block), block), :] = wide_ref[pl.ds(j * lap, block), :].astype(BF)
        copy_out(j).start()
        return carry

    lax.fori_loop(0, NJ, narrow, 0)

    def drain(j, carry):
        copy_out(j).wait()
        return carry

    lax.fori_loop(0, NJ, drain, 0)


def fft_kernel(n_out, n_parts, slots, taps_a, taps_b, mask_ref, v_hbm, *refs):
    parts, refs = refs[:n_parts], refs[n_parts:]
    w_ref, tw_ref, table_ref, out_ref, v_buf, hist_buf, sections, zhi, zlo, wide, slabs, sems, out_sems = refs
    keep = mask_ref[0].astype(F32)
    groups = v_buf.shape[0] // 16

    def copies(g, side):
        rows = pl.ds(pl.multiple_of(g * 16, 16), 16)
        jobs = [pltpu.make_async_copy(v_hbm.at[rows], v_buf.at[rows], sems.at[0, g])]
        for k, slot in enumerate(slots):
            part, skip = slot[side]
            source = parts[part].at[pl.ds(pl.multiple_of((g + skip) * 16, 16), 16)]
            jobs.append(pltpu.make_async_copy(source, hist_buf.at[k, rows], sems.at[k + 1, g]))
        return jobs

    for g in range(groups):
        for job in copies(g, g // (groups // 2)):
            job.start()

    def run(taps, side):
        def body(g, carry):
            for job in copies(g, side):
                job.wait()
            rows = pl.ds(pl.multiple_of(g * 16, 16), 16)

            def frames_of(n1, w):
                lanes = slice(n1 * N2, (n1 + 1) * N2)
                v = [v_buf[rows, i * NFFT + n1 * N2 : i * NFFT + (n1 + 1) * N2].astype(F32) for i in range(3)]
                h = [hist_buf[k, rows, lanes].astype(F32) for k in range(len(slots))]
                return taps(keep, w, v, h)

            sections_of(frames_of, n_out, w_ref, sections)
            for f in range(n_out):
                at = pl.multiple_of(f * N2 + g * 16, 16)
                first_half_bins(sections, tw_ref, zhi, zlo, f, pl.ds(at, 16))
            return carry

        return body

    lax.fori_loop(0, groups // 2, run(taps_a, 0), 0)
    lax.fori_loop(groups // 2, groups, run(taps_b, 1), 0)
    emit_slabs(n_out, table_ref, zhi, zlo, wide, slabs, out_ref, out_sems)


def first_a(keep, w, v, h):
    return (w[0] * h[0] + w[1] * v[0] + w[2] * v[1] + w[3] * v[2],)


def first_b(keep, w, v, h):
    return (keep * (w[0] * v[0] + w[1] * v[1] + w[2] * v[2]) + w[3] * h[0],)


def second_a(keep, w, v, h):
    near, one_off, two_off = h
    return (
        keep * (w[0] * v[0] + w[1] * v[1] + w[2] * v[2]) + w[3] * one_off,
        w[0] * two_off + w[1] * near + w[2] * v[0] + w[3] * v[1],
    )


def second_b(keep, w, v, h):
    near, one_off, two_off = h
    return (
        w[0] * one_off + w[1] * v[0] + w[2] * v[1] + w[3] * v[2],
        keep * (w[0] * v[1] + w[1] * v[2]) + w[2] * near + w[3] * two_off,
    )


def spectra_call(n_out, taps_a, taps_b, mask, voltages, parts, slots, window):
    signals = voltages.shape[0]
    n_hist = len(slots)
    rows = CH * 2 * n_out
    vmem = pl.BlockSpec(memory_space=pltpu.VMEM)
    hbm = pl.BlockSpec(memory_space=pltpu.HBM)
    return pl.pallas_call(
        lambda *refs: fft_kernel(n_out, len(parts), slots, taps_a, taps_b, *refs),
        out_shape=jax.ShapeDtypeStruct((rows, N2), BF),
        in_specs=[pl.BlockSpec(memory_space=pltpu.SMEM), hbm] + [hbm] * len(parts) + [vmem] * 3,
        out_specs=hbm,
        scratch_shapes=[
            pltpu.VMEM(voltages.shape, BF),
            pltpu.VMEM((n_hist, signals, NFFT), BF),
            pltpu.VMEM((n_out, 8, 8, 16, N2), F32),
            pltpu.VMEM((NK, n_out * N2, 2 * N2), BF),
            pltpu.VMEM((NK, n_out * N2, 2 * N2), BF),
            pltpu.VMEM((rows + NJ, N2), F32),
            pltpu.VMEM((rows, N2), BF),
            pltpu.SemaphoreType.DMA((n_hist + 1, signals // 16)),
            pltpu.SemaphoreType.DMA((NJ,)),
        ],
        cost_estimate=pl.CostEstimate(flops=n_out * 10**10, transcendentals=0, bytes_accessed=n_out * 10**7),
        compiler_params=pltpu.CompilerParams(vmem_limit_bytes=56 * 1024 * 1024),
    )(mask, voltages, *parts, window, jnp.asarray(twiddle_table()), jnp.asarray(bin_table()))


LAP = 2 * N2 + 1


def spread_kernel(in_ref, out_ref, wide):
    def body(t, carry):
        for src in range(2):
            tile = in_ref[pl.ds(pl.multiple_of((t * 2 + src) * 16, 16), 16), :].astype(F32)
            for part in range(2):
                wide[src, pl.ds(part * N2 + t, 8, stride=LAP), :] = tile[part * 8 : part * 8 + 8]
        return carry

    lax.fori_loop(0, N2, body, 0)
    for ch in range(8):
        for src in range(2):
            out_ref[ch, :, src * N2 : (src + 1) * N2] = wide[src, ch * LAP : ch * LAP + 2 * N2, :].astype(BF)


def spread(first):
    vmem = pl.BlockSpec(memory_space=pltpu.VMEM)
    return pl.pallas_call(
        spread_kernel,
        out_shape=jax.ShapeDtypeStruct((8, 2 * N2, 2 * N2), BF),
        in_specs=[vmem],
        out_specs=vmem,
        scratch_shapes=[pltpu.VMEM((2, 8 * LAP + 8, N2), F32)],
        cost_estimate=pl.CostEstimate(flops=2 * 10**9, transcendentals=0, bytes_accessed=10**6),
        compiler_params=pltpu.CompilerParams(vmem_limit_bytes=16 * 1024 * 1024),
    )(first)


def correlate_kernel(own_ref, first_ref, second_ref, out_hbm, send_ref, wide, real, imag, rows_buf, sems):
    own = own_ref[0]
    scale = 1.0 / math.sqrt(3 * N2)
    first_lanes = lax.broadcasted_iota(jnp.int32, (16, N2), 1) < N2 // 2

    def body(t, carry):
        for src in range(2):
            for f in range(2):
                row = pl.multiple_of((t * 2 + src) * 32 + f * 16, 16)
                tile = second_ref[pl.ds(row, 16), :].astype(F32)
                if f:
                    row = pl.multiple_of(((t + N2 - 1) % N2 * 2 + src) * 32 + 16, 16)
                    tile = jnp.where(first_lanes, tile, second_ref[pl.ds(row, 16), :].astype(F32))
                for part in range(2):
                    wide[f, src, pl.ds(part * N2 + t, 8, stride=LAP), :] = tile[part * 8 : part * 8 + 8]
        return carry

    lax.fori_loop(0, N2, body, 0)

    first = own == 0
    mine = pl.ds(pl.multiple_of(own * N2, N2), N2)
    theirs = pl.ds(pl.multiple_of((1 - own) * N2, N2), N2)
    upper = lax.broadcasted_iota(jnp.int32, (N2, N2), 0) <= lax.broadcasted_iota(jnp.int32, (N2, N2), 1)
    half_lanes = lax.broadcasted_iota(jnp.int32, (2 * N2, 2 * N2), 1) % N2 < N2 // 2
    dims = (((0,), (0,)), ((), ()))

    def copy_out(ch):
        return pltpu.make_async_copy(rows_buf.at[ch], out_hbm.at[own * 8 + ch], sems.at[ch])

    for ch in range(8):
        rows = slice(ch * LAP, ch * LAP + 2 * N2)
        g1, g2 = (
            jnp.concatenate([wide[f, 0, rows, :].astype(BF), wide[f, 1, rows, :].astype(BF)], axis=1)
            for f in range(2)
        )
        g0 = first_ref[ch]
        x = [jnp.where(half_lanes, g0, g1), jnp.where(half_lanes, g1, g0), g2]
        xr = jnp.concatenate([part[:N2] for part in x], axis=0)
        xi = jnp.concatenate([part[N2:] for part in x], axis=0)
        both = jnp.concatenate([xr, xi], axis=0)
        p = lax.dot_general(xi, xr, dims, preferred_element_type=F32) * scale
        real[...] = lax.dot_general(both, both, dims, preferred_element_type=F32) * scale
        imag[...] = p - p.T
        rows_buf[ch, :, : 2 * N2] = real[mine, :]
        rows_buf[ch, :, 2 * N2 :] = imag[mine, :]
        copy_out(ch).start()
        rows_r, rows_i = real[theirs, :], imag[theirs, :]
        cross_r = jnp.where(first, rows_r[:, :N2], rows_r[:, N2:])
        cross_i = jnp.where(first, rows_i[:, :N2], rows_i[:, N2:])
        diag_r = jnp.where(first, rows_r[:, N2:], rows_r[:, :N2])
        diag_i = jnp.where(first, rows_i[:, N2:], rows_i[:, :N2])
        send_ref[ch, :, :N2] = cross_r.astype(BF)
        send_ref[ch, :, N2 : 2 * N2] = cross_i.astype(BF)
        send_ref[ch, :, 2 * N2 :] = jnp.where(upper, diag_r, diag_i).astype(BF)

    for ch in range(8):
        copy_out(ch).wait()


def correlate(own, first, second):
    vmem = pl.BlockSpec(memory_space=pltpu.VMEM)
    return pl.pallas_call(
        correlate_kernel,
        out_shape=[
            jax.ShapeDtypeStruct((16, N2, 4 * N2), F32),
            jax.ShapeDtypeStruct((8, N2, 3 * N2), BF),
        ],
        in_specs=[pl.BlockSpec(memory_space=pltpu.SMEM), vmem, vmem],
        out_specs=[pl.BlockSpec(memory_space=pltpu.HBM), vmem],
        scratch_shapes=[
            pltpu.VMEM((2, 2, 8 * LAP + 8, N2), F32),
            pltpu.VMEM((2 * N2, 2 * N2), F32),
            pltpu.VMEM((2 * N2, 2 * N2), F32),
            pltpu.VMEM((8, N2, 4 * N2), F32),
            pltpu.SemaphoreType.DMA((8,)),
        ],
        cost_estimate=pl.CostEstimate(flops=5 * 10**9, transcendentals=0, bytes_accessed=10**7),
        compiler_params=pltpu.CompilerParams(vmem_limit_bytes=40 * 1024 * 1024),
    )(own, first, second)


def finish_kernel(own_ref, part_ref, got_ref, out_hbm, rows_buf, sems):
    own = own_ref[0]
    first = own == 0
    row = lax.broadcasted_iota(jnp.int32, (N2, N2), 0)
    col = lax.broadcasted_iota(jnp.int32, (N2, N2), 1)

    def copy_out(ch):
        return pltpu.make_async_copy(rows_buf.at[ch], out_hbm.at[(1 - own) * 8 + ch], sems.at[ch])

    for ch in range(8):
        cross_r = got_ref[ch, :, :N2].astype(F32)
        cross_i = got_ref[ch, :, N2 : 2 * N2].astype(F32)
        packed = got_ref[ch, :, 2 * N2 :].astype(F32)
        flipped = packed.T
        diag_r = jnp.where(row <= col, packed, flipped)
        diag_i = jnp.where(row > col, packed, jnp.where(row < col, -flipped, 0.0))
        rows_buf[ch, :, :N2] = jnp.where(first, diag_r, cross_r)
        rows_buf[ch, :, N2 : 2 * N2] = jnp.where(first, cross_r, diag_r)
        rows_buf[ch, :, 2 * N2 : 3 * N2] = jnp.where(first, diag_i, cross_i)
        rows_buf[ch, :, 3 * N2 :] = jnp.where(first, cross_i, diag_i)
        copy_out(ch).start()
    for ch in range(8):
        copy_out(ch).wait()


def finish(own, part, got):
    return pl.pallas_call(
        finish_kernel,
        out_shape=jax.ShapeDtypeStruct(part.shape, F32),
        in_specs=[
            pl.BlockSpec(memory_space=pltpu.SMEM),
            pl.BlockSpec(memory_space=pltpu.HBM),
            pl.BlockSpec(memory_space=pltpu.VMEM),
        ],
        out_specs=pl.BlockSpec(memory_space=pltpu.HBM),
        scratch_shapes=[pltpu.VMEM((8, N2, 4 * N2), F32), pltpu.SemaphoreType.DMA((8,))],
        input_output_aliases={1: 0},
        compiler_params=pltpu.CompilerParams(vmem_limit_bytes=8 * 1024 * 1024),
    )(own, part, got)


def cut_kernel(plan, v_hbm, *refs):
    outs, sems = refs[: len(plan)], refs[len(plan)]
    jobs = []
    for out, pieces in zip(outs, plan):
        at = 0
        for (start, stop), frame in pieces:
            for row in range(start, stop, 16):
                source = v_hbm.at[pl.ds(row, 16), pl.ds(frame * NFFT, NFFT)]
                jobs.append(pltpu.make_async_copy(source, out.at[pl.ds(at, 16)], sems.at[len(jobs)]))
                at += 16
    for job in jobs:
        job.start()
    for job in jobs:
        job.wait()


def cut(voltages, plan):
    sizes = [sum(stop - start for (start, stop), _ in pieces) for pieces in plan]
    hbm = pl.BlockSpec(memory_space=pltpu.HBM)
    return pl.pallas_call(
        lambda *refs: cut_kernel(plan, *refs),
        out_shape=[jax.ShapeDtypeStruct((size, NFFT), BF) for size in sizes],
        in_specs=[hbm],
        out_specs=[pl.BlockSpec(memory_space=pltpu.VMEM)] * len(plan),
        scratch_shapes=[pltpu.SemaphoreType.DMA((sum(sizes) // 16,))],
        cost_estimate=pl.CostEstimate(flops=10**9, transcendentals=0, bytes_accessed=10**7),
        compiler_params=pltpu.CompilerParams(vmem_limit_bytes=60 * 1024 * 1024),
    )(voltages)


def per_device(voltages, pfb_window):
    signals = voltages.shape[0]
    peers = lax.axis_size("ta")
    half = signals // 2
    to_right = [(i, i + 1) for i in range(peers - 1)]
    to_left = [(i, (i - 1) % peers) for i in range(peers)]
    inner = (lax.axis_index("ta") < peers - 1).astype(jnp.int32).reshape(1)
    own = lax.axis_index("aa").astype(jnp.int32).reshape(1)
    to_r, to_l = cut(voltages, ((((0, half), 2),), (((half, signals), 0),)))
    prev_a = lax.ppermute(to_r, "ta", to_right)
    next_b = lax.ppermute(to_l, "ta", to_left)
    top, bottom = (0, half), (half, signals)
    to_r, to_l = cut(voltages, (((top, 1), (bottom, 2)), ((top, 0), (bottom, 1))))
    right = lax.ppermute(to_r, "ta", to_right)
    left = lax.ppermute(to_l, "ta", to_left)
    low = -(half // 16)
    near = ((0, 0), (1, low))
    first = spectra_call(1, first_a, first_b, inner, voltages, (prev_a, next_b), (near,), pfb_window)
    first = lax.all_to_all(first, ("ta", "aa"), split_axis=0, concat_axis=0, tiled=True)
    slots = (near, ((2, 0), (3, 0)), ((3, 0), (2, 0)))
    parts = (prev_a, next_b, left, right)
    second = spectra_call(2, second_a, second_b, inner, voltages, parts, slots, pfb_window)
    second = lax.all_to_all(second, ("ta", "aa"), split_axis=0, concat_axis=0, tiled=True)
    first = spread(first)
    part, send = correlate(own, first, second)
    got = lax.ppermute(send, "aa", [(0, 1), (1, 0)])
    return finish(own, part, got)


def solution(mesh):
    return jax.shard_map(
        per_device,
        mesh=mesh,
        in_specs=(P("aa", "ta"), P()),
        out_specs=P("ta", "aa", None),
        check_vma=False,
    )
```

time: 211 us -> 170 us (0.81)
  waiting for transfers between devices: 105 us -> 80.2 us
  Pallas kernels: 59.3 us -> 51.2 us
  local copies, waits for them, and re-layouts: 7.84 us -> 4.46 us
  other arithmetic: 2.73 us -> 0 us
    ppermute x4, waiting for transfers between devices: 29.4 us -> 5.85 us  [the longest x1 5.8 us: per_device(): prev_a = lax.ppermute(to_r, 'ta', to_right)]
    pallas_call x1, Pallas kernels: 11.9 us -> 4.79 us  [correlate(): pl.pallas_call(correlate_kernel, out_shape=[jax.ShapeDtypeStruct((16, N2,...]
    slice x2 -> x0, local copies, waits for them, and re-layouts: 6.95 us -> none  [the longest x1 3.9 us: per_device(): following = lax.ppermute(voltages[:, :NFFT], 'ta', to_left)]
    pallas_call x1, Pallas kernels: 5.65 us -> 1.57 us  [finish(): pl.pallas_call(finish_kernel, out_shape=jax.ShapeDtypeStruct(part.shape,...]
    unnamed x2 -> x8, local copies, waits for them, and re-layouts: 0.88 us -> 4.46 us
    pallas_call x2 -> x5, Pallas kernels: 41.7 us -> 44.8 us  [the longest x2 36.6 us: spectra_call(): pl.pallas_call(lambda *refs: fft_kernel(n_out, len(parts), slots, taps_a,...]
    concatenate x1 -> x0, other arithmetic: 2.73 us -> none  [per_device(): side = jnp.concatenate([prev_side, next_side], axis=0)]
  transfers between devices with their start and end apart: 7 -> 7, of which waited for: 4 -> 4; matrix products, arithmetic and copies ran while one was open for 3% -> 0% of each run, Pallas kernels for 11% -> 25%
where the time goes in v1:
time: 170 us; the launch traced here: 168 us
  waiting for transfers between devices  80.2 us (47%)
  Pallas kernels  51.2 us (30%)
  starting transfers between devices  31.6 us (19%)
  local copies, waits for them, and re-layouts  4.46 us (3%)
    all_to_all x1, waiting for transfers between devices, per_device(): lax.all_to_all(second, ('ta', 'aa'), split_axis=0, concat_axis=0, tiled=T...  48.5 us
    pallas_call x2, Pallas kernels, spectra_call(): pl.pallas_call(lambda *refs: fft_kernel(n_out, len(parts), slots, taps_a,...  36.6 us
    ppermute x1, waiting for transfers between devices, per_device(): got = lax.ppermute(send, 'aa', [(0, 1), (1, 0)])  19.4 us
    all_to_all x1, starting transfers between devices, per_device(): lax.all_to_all(first, ('ta', 'aa'), split_axis=0, concat_axis=0, tiled=True)  15.5 us
    all_to_all x1, starting transfers between devices, per_device(): lax.all_to_all(second, ('ta', 'aa'), split_axis=0, concat_axis=0, tiled=T...  8.14 us
    pallas_call x2, Pallas kernels, cut(): pl.pallas_call(lambda *refs: cut_kernel(plan, *refs), out_shape=[jax.Shap...  7.2 us
    all_to_all x1, waiting for transfers between devices, per_device(): lax.all_to_all(first, ('ta', 'aa'), split_axis=0, concat_axis=0, tiled=True)  6.39 us
    ppermute x1, waiting for transfers between devices, per_device(): prev_a = lax.ppermute(to_r, 'ta', to_right)  5.8 us
  transfers between devices with their start and end apart: 7, of which 4 were waited for; matrix products, arithmetic and copies ran while one was open for 0% of the time, Pallas kernels for 25%

profile of v1, /device:TPU:64, one launch (start us, length us, event | category | flops | bytes accessed | tf_op | source)
XLA Modules:
  0.0 167.5 jit_solution(522158071536622948)
XLA Ops:
  0.0 2.9 %shard_map.64 = (bf16[64,8192]{1,0:T(8,128)(2,1)}, bf16[64,8192]{1,0:T(8,128)(2,1)}) custom-call(bf16[128,24576]{1,0:T(8,128)(2,1)} %refs_1_.3), custom_call_target="tpu_custom_call" | custom-call | flops 1000000000 | bytes 10000000 | tf_op jit(solution)/shard_map/pallas_call | solution.py:450
  2.9 1.9 %collective-permute-start = (bf16[64,8192]{1,0:T(8,128)(2,1)}, bf16[64,8192]{1,0:T(8,128)(2,1)S(1)}, u32[]{:S(2)}, u32[]{:S(2)}) collective-permute-start(bf16[64,8192]{1,0:T(8,128)(2,1)} %get-tuple-element.11), channel_id=1, source_target_pairs={{0,2},{2,4},{4,6},{6,8},{8,10},{10,12},{12,14},{14,16},{16,18},{18... | collective-permute-start | bytes 3145736 | tf_op jit(solution)/shard_map/ppermute | solution.py:470
  4.9 1.8 %collective-permute-start.1 = (bf16[64,8192]{1,0:T(8,128)(2,1)}, bf16[64,8192]{1,0:T(8,128)(2,1)}, u32[]{:S(2)}, u32[]{:S(2)}) collective-permute-start(bf16[64,8192]{1,0:T(8,128)(2,1)} %get-tuple-element.12), channel_id=1, source_target_pairs={{0,254},{2,0},{4,2},{6,4},{8,6},{10,8},{12,10},{14,12},{16,14},{18... | collective-permute-start | bytes 3145736 | tf_op jit(solution)/shard_map/ppermute | solution.py:471
  6.7 4.3 %shard_map.67 = (bf16[128,8192]{1,0:T(8,128)(2,1)}, bf16[128,8192]{1,0:T(8,128)(2,1)}) custom-call(bf16[128,24576]{1,0:T(8,128)(2,1)} %refs_1_.3), custom_call_target="tpu_custom_call" | custom-call | flops 1000000000 | bytes 10000000 | tf_op jit(solution)/shard_map/pallas_call | solution.py:450
  11.0 0.1 collective-permute-start.2
  11.1 2.4 %collective-permute-start.3 = (bf16[128,8192]{1,0:T(8,128)(2,1)}, bf16[128,8192]{1,0:T(8,128)(2,1)}, u32[]{:S(2)}, u32[]{:S(2)}) collective-permute-start(bf16[128,8192]{1,0:T(8,128)(2,1)} %get-tuple-element.14), channel_id=1, source_target_pairs={{0,2},{2,4},{4,6},{6,8},{8,10},{10,12},{12,14},{14,16},{16,18},{18... | collective-permute-start | bytes 6291464 | tf_op jit(solution)/shard_map/ppermute | solution.py:474
  13.5 5.8 %collective-permute-done.refs_2_ = bf16[64,8192]{1,0:T(8,128)(2,1)S(1)} collective-permute-done((bf16[64,8192]{1,0:T(8,128)(2,1)}, bf16[64,8192]{1,0:T(8,128)(2,1)S(1)}, u32[]{:S(2)}, u32[]{:S(2)}) %collective-permute-start) | collective-permute-done | bytes 1048608 | tf_op jit(solution)/shard_map/ppermute | solution.py:470
  19.3 0.0 collective-permute-done.1.refs_3_
  19.3 1.0 copy-done.3
  20.3 15.5 %shard_map.65 = bf16[4096,128]{1,0:T(8,128)(2,1)} custom-call(s32[1]{0:T(128)} %bitcast.1.refs_0_, bf16[128,24576]{1,0:T(8,128)(2,1)} %refs_1_.3, bf16[64,8192]{1,0:T(8,128)(2,1)} %copy-done.3, bf16[64,8192]{1,0:T(8,128)(2,1)} %collective-permute-done.1.refs_3_, f32[4,8192]{1,0:T(4,128)} %refs_6_.2, f32[33,2,128]{2,1,0:T(2,128)} %constant.14.clone.refs_5_.refs_7_, ...), custom_call_target="tpu_custom_call" | custom-call | flops 10000000000 | bytes 10000000 | tf_op jit(solution)/shard_map/pallas_call | solution.py:258
  35.8 15.5 %all-to-all-start = ((bf16[256,16,128]{2,1,0:T(8,128)(2,1)}), bf16[256,16,128]{2,1,0:T(8,128)(2,1)S(1)}, u32[]{:S(2)}, u32[]{:S(2)}) async-start(bf16[256,16,128]{2,1,0:T(8,128)(2,1)} %bitcast.9), calls=%async_computation | async-start | bytes 2097152 | tf_op jit(solution)/shard_map/all_to_all | solution.py:479
  51.3 0.0 collective-permute-done.2.refs_4_
  51.3 1.3 copy-done.2
  52.6 21.1 %shard_map.68 = bf16[8192,128]{1,0:T(8,128)(2,1)} custom-call(s32[1]{0:T(128)} %bitcast.1.refs_0_, bf16[128,24576]{1,0:T(8,128)(2,1)} %refs_1_.3, bf16[64,8192]{1,0:T(8,128)(2,1)} %copy-done.3, bf16[64,8192]{1,0:T(8,128)(2,1)} %collective-permute-done.1.refs_3_, bf16[128,8192]{1,0:T(8,128)(2,1)} %copy-done.2, ...), custom_call_target="tpu_custom_call" | custom-call | flops 20000000000 | bytes 20000000 | tf_op jit(solution)/shard_map/pallas_call | solution.py:258
  73.7 6.4 %all-to-all-done = bf16[256,16,128]{2,1,0:T(8,128)(2,1)S(1)} async-done(((bf16[256,16,128]{2,1,0:T(8,128)(2,1)}), bf16[256,16,128]{2,1,0:T(8,128)(2,1)S(1)}, u32[]{:S(2)}, u32[]{:S(2)}) %all-to-all-start) | async-done | bytes 1048608 | tf_op jit(solution)/shard_map/all_to_all | solution.py:479
  80.1 8.1 %all-to-all-start.1 = ((bf16[256,32,128]{2,1,0:T(8,128)(2,1)}), bf16[256,32,128]{2,1,0:T(8,128)(2,1)S(1)}, u32[]{:S(2)}, u32[]{:S(2)}) async-start(bf16[256,32,128]{2,1,0:T(8,128)(2,1)} %bitcast.8), calls=%async_computation.1 | async-start | bytes 4194304 | tf_op jit(solution)/shard_map/all_to_all | solution.py:483
  88.2 1.1 shard_map.66.first_ref
  89.3 1.0 copy-done
  90.3 48.5 %all-to-all-done.1 = bf16[256,32,128]{2,1,0:T(8,128)(2,1)S(1)} async-done(((bf16[256,32,128]{2,1,0:T(8,128)(2,1)}), bf16[256,32,128]{2,1,0:T(8,128)(2,1)S(1)}, u32[]{:S(2)}, u32[]{:S(2)}) %all-to-all-start.1) | async-done | bytes 2097184 | tf_op jit(solution)/shard_map/all_to_all | solution.py:483
  138.8 1.2 copy-done.1
  140.0 4.8 %shard_map.69 = (f32[16,128,512]{2,1,0:T(8,128)}, bf16[8,128,384]{2,1,0:T(8,128)(2,1)S(1)}) custom-call(s32[1]{0:T(128)} %bitcast.own_ref, bf16[8,256,256]{2,1,0:T(8,128)(2,1)S(1)} %copy-done.1, bf16[8192,128]{1,0:T(8,128)(2,1)S(1)} %bitcast.6), custom_call_target="tpu_custom_call" | custom-call | flops 5000000000 | bytes 10000000 | tf_op jit(solution)/shard_map/pallas_call | solution.py:370
  144.8 1.7 %collective-permute-start.4 = (bf16[8,128,384]{2,1,0:T(8,128)(2,1)S(1)}, bf16[8,128,384]{2,1,0:T(8,128)(2,1)S(1)}, u32[]{:S(2)}, u32[]{:S(2)}) collective-permute-start(bf16[8,128,384]{2,1,0:T(8,128)(2,1)S(1)} %get-tuple-element.16), channel_id=1, source_target_pairs={{0,1},{1,0},{2,3},{3,2},{4,5},{5,4},{6,7},{7,6},{8,9},{9,8},{10,11... | collective-permute-start | bytes 2359304 | tf_op jit(solution)/shard_map/ppermute | solution.py:486
  146.5 19.4 %collective-permute-done.4.got_ref = bf16[8,128,384]{2,1,0:T(8,128)(2,1)S(1)} collective-permute-done((bf16[8,128,384]{2,1,0:T(8,128)(2,1)S(1)}, bf16[8,128,384]{2,1,0:T(8,128)(2,1)S(1)}, u32[]{:S(2)}, u32[]{:S(2)}) %collective-permute-start.4) | collective-permute-done | bytes 786464 | tf_op jit(solution)/shard_map/ppermute | solution.py:486
  166.0 1.6 shard_map.70
  (5 shorter events, 0.0 us)
Async XLA Ops:
  2.9 16.3 %collective-permute-start = (bf16[64,8192]{1,0:T(8,128)(2,1)}, bf16[64,8192]{1,0:T(8,128)(2,1)S(1)}, u32[]{:S(2)}, u32[]{:S(2)}) collective-permute-start(bf16[64,8192]{1,0:T(8,128)(2,1)} %get-tuple-element.11), channel_id=1, source_target_pairs={{0,2},{2,4},{4,6},{6,8},{8,10},{10,12},{12,14},{14,16},{16,18},{18... | collective-permute-start | bytes 3145736 | tf_op jit(solution)/shard_map/ppermute | solution.py:470
  4.9 14.4 %collective-permute-start.1 = (bf16[64,8192]{1,0:T(8,128)(2,1)}, bf16[64,8192]{1,0:T(8,128)(2,1)}, u32[]{:S(2)}, u32[]{:S(2)}) collective-permute-start(bf16[64,8192]{1,0:T(8,128)(2,1)} %get-tuple-element.12), channel_id=1, source_target_pairs={{0,254},{2,0},{4,2},{6,4},{8,6},{10,8},{12,10},{14,12},{16,14},{18... | collective-permute-start | bytes 3145736 | tf_op jit(solution)/shard_map/ppermute | solution.py:471
  11.0 40.3 %collective-permute-start.2 = (bf16[128,8192]{1,0:T(8,128)(2,1)}, bf16[128,8192]{1,0:T(8,128)(2,1)S(1)}, u32[]{:S(2)}, u32[]{:S(2)}) collective-permute-start(bf16[128,8192]{1,0:T(8,128)(2,1)} %get-tuple-element.13), channel_id=1, source_target_pairs={{0,254},{2,0},{4,2},{6,4},{8,6},{10,8},{12,10},{14,12},{16,14},{18... | collective-permute-start | bytes 6291464 | tf_op jit(solution)/shard_map/ppermute | solution.py:475
  11.1 40.2 %collective-permute-start.3 = (bf16[128,8192]{1,0:T(8,128)(2,1)}, bf16[128,8192]{1,0:T(8,128)(2,1)}, u32[]{:S(2)}, u32[]{:S(2)}) collective-permute-start(bf16[128,8192]{1,0:T(8,128)(2,1)} %get-tuple-element.14), channel_id=1, source_target_pairs={{0,2},{2,4},{4,6},{6,8},{8,10},{10,12},{12,14},{14,16},{16,18},{18... | collective-permute-start | bytes 6291464 | tf_op jit(solution)/shard_map/ppermute | solution.py:474
  19.3 1.0 copy-start.3
  35.8 44.3 %all-to-all-start = ((bf16[256,16,128]{2,1,0:T(8,128)(2,1)}), bf16[256,16,128]{2,1,0:T(8,128)(2,1)S(1)}, u32[]{:S(2)}, u32[]{:S(2)}) async-start(bf16[256,16,128]{2,1,0:T(8,128)(2,1)} %bitcast.9), calls=%async_computation | async-start | bytes 2097152 | tf_op jit(solution)/shard_map/all_to_all | solution.py:479
  51.3 1.3 copy-start.2
  80.1 58.7 %all-to-all-start.1 = ((bf16[256,32,128]{2,1,0:T(8,128)(2,1)}), bf16[256,32,128]{2,1,0:T(8,128)(2,1)S(1)}, u32[]{:S(2)}, u32[]{:S(2)}) async-start(bf16[256,32,128]{2,1,0:T(8,128)(2,1)} %bitcast.8), calls=%async_computation.1 | async-start | bytes 4194304 | tf_op jit(solution)/shard_map/all_to_all | solution.py:483
  89.3 1.0 copy-start
  138.8 1.2 copy-start.1
  144.8 21.2 %collective-permute-start.4 = (bf16[8,128,384]{2,1,0:T(8,128)(2,1)S(1)}, bf16[8,128,384]{2,1,0:T(8,128)(2,1)S(1)}, u32[]{:S(2)}, u32[]{:S(2)}) collective-permute-start(bf16[8,128,384]{2,1,0:T(8,128)(2,1)S(1)} %get-tuple-element.16), channel_id=1, source_target_pairs={{0,1},{1,0},{2,3},{3,2},{4,5},{5,4},{6,7},{7,6},{8,9},{9,8},{10,11... | collective-permute-start | bytes 2359304 | tf_op jit(solution)/shard_map/ppermute | solution.py:486

commit v2 on v1

--- a/solution.py
+++ b/solution.py
@@ -18,6 +18,7 @@
 NJ = CH // N1
 K2 = CH_OFF // N1
 HALF = math.sqrt(0.5)
+UNROLL = 32
 BF = jnp.bfloat16
 F32 = jnp.float32
 
@@ -39,7 +40,7 @@
     table = np.concatenate(rows, axis=0)
     high = table.astype(BF)
     low = (table - high.astype(np.float64)).astype(BF)
-    return np.concatenate([high, low], axis=0)
+    return np.concatenate([high, low], axis=0).T
 
 
 def real_dft8(x):
@@ -76,7 +77,9 @@
     return out
 
 
-def first_half_bins(sections, tw_ref, zhi_ref, zlo_ref, frame, rows):
+def first_half_bins(sections, tw_ref, z_ref, frame, row):
+    low_row = row + z_ref.shape[1] // 2
+
     def keep(k1, re, im, conj):
         c, s = tw_ref[k1, 0:1, :], tw_ref[k1, 1:2, :]
         if im is None:
@@ -88,8 +91,9 @@
         for part, z in ((0, zr), (1, zi)):
             high = z.astype(BF)
             low = (z - high.astype(F32)).astype(BF)
-            zhi_ref[k1, rows, part * N2 : (part + 1) * N2] = high
-            zlo_ref[k1, rows, part * N2 : (part + 1) * N2] = low
+            lanes = slice(part * N2, (part + 1) * N2)
+            z_ref[k1, pl.ds(pl.multiple_of(row, 16), 16), lanes] = high
+            z_ref[k1, pl.ds(pl.multiple_of(low_row, 16), 16), lanes] = low
 
     spectrum = real_dft8([sections[frame, 0, b] for b in range(8)])
     for r in range(5):
@@ -135,33 +139,30 @@
             sections[f, 7, b] = spectrum[4][0]
 
 
-def emit_slabs(n_out, table_ref, zhi_ref, zlo_ref, wide_ref, slabs_ref, out_ref, out_sems):
+def emit_slabs(n_out, table_ref, z_ref, wide_ref, slabs_ref, out_ref, out_sems):
     slab = n_out * 16
     block = 8 * slab
     lap = block + 1
-
-    def one(k1, mirror):
-        dims = (((1,), (1,)), ((), ()))
-        both = lax.dot_general(table_ref[...], zhi_ref[k1], dims, preferred_element_type=F32)
-        more = lax.dot_general(table_ref[0:N2, :], zlo_ref[k1], dims, preferred_element_type=F32)
-        spectrum = both[:N2] + both[N2:] + more
-        for side in range(2 if mirror else 1):
-            ch = N1 - k1 if side else k1
-            start = (ch // 8) * slab + ch % 8
-            for part in range(2):
-                at = (side * 2 + part) * NJ
-                for f in range(n_out):
-                    wide_ref[pl.ds(start + (f * 2 + part) * 8, NJ, stride=lap), :] = spectrum[
-                        at : at + NJ, f * N2 : (f + 1) * N2
-                    ]
-
-    one(0, False)
-
-    def body(k1, carry):
-        one(k1, True)
-        return carry
-
-    lax.fori_loop(1, NK, body, 0)
+    rows = n_out * N2
+
+    def some(first, count, mirror):
+        left = z_ref[pl.ds(first, count)].reshape(count * 2 * rows, 2 * N2)
+        product = jnp.dot(left, table_ref[...], preferred_element_type=F32)
+        for u in range(count):
+            k1 = first + u
+            high, low = (product[(2 * u + i) * rows : (2 * u + i + 1) * rows] for i in range(2))
+            spectrum = high[:, :N2] + high[:, N2:] + low[:, :N2]
+            for f in range(n_out):
+                flipped = spectrum[f * N2 : (f + 1) * N2].T
+                for side in range(2 if mirror else 1):
+                    ch = N1 - k1 if side else k1
+                    start = (ch >> 3) * slab + (ch & 7) + f * 16
+                    for part in range(2):
+                        at = (side * 2 + part) * NJ
+                        wide_ref[pl.ds(start + part * 8, NJ, stride=lap), :] = flipped[at : at + NJ]
+
+    some(0, 1, False)
+    lax.fori_loop(0, (NK - 1) // UNROLL, lambda i, c: (some(1 + i * UNROLL, UNROLL, True), c)[1], 0)
 
     def copy_out(j):
         rows = pl.ds(pl.multiple_of(j * block, block), block)
@@ -183,7 +184,7 @@
 
 def fft_kernel(n_out, n_parts, slots, taps_a, taps_b, mask_ref, v_hbm, *refs):
     parts, refs = refs[:n_parts], refs[n_parts:]
-    w_ref, tw_ref, table_ref, out_ref, v_buf, hist_buf, sections, zhi, zlo, wide, slabs, sems, out_sems = refs
+    w_ref, tw_ref, table_ref, out_ref, v_buf, hist_buf, sections, z, wide, slabs, sems, out_sems = refs
     keep = mask_ref[0].astype(F32)
     groups = v_buf.shape[0] // 16
 
@@ -214,15 +215,14 @@
 
             sections_of(frames_of, n_out, w_ref, sections)
             for f in range(n_out):
-                at = pl.multiple_of(f * N2 + g * 16, 16)
-                first_half_bins(sections, tw_ref, zhi, zlo, f, pl.ds(at, 16))
+                first_half_bins(sections, tw_ref, z, f, f * N2 + g * 16)
             return carry
 
         return body
 
     lax.fori_loop(0, groups // 2, run(taps_a, 0), 0)
     lax.fori_loop(groups // 2, groups, run(taps_b, 1), 0)
-    emit_slabs(n_out, table_ref, zhi, zlo, wide, slabs, out_ref, out_sems)
+    emit_slabs(n_out, table_ref, z, wide, slabs, out_ref, out_sems)
 
 
 def first_a(keep, w, v, h):
@@ -264,15 +264,14 @@
             pltpu.VMEM(voltages.shape, BF),
             pltpu.VMEM((n_hist, signals, NFFT), BF),
             pltpu.VMEM((n_out, 8, 8, 16, N2), F32),
-            pltpu.VMEM((NK, n_out * N2, 2 * N2), BF),
-            pltpu.VMEM((NK, n_out * N2, 2 * N2), BF),
+            pltpu.VMEM((NK, 2 * n_out * N2, 2 * N2), BF),
             pltpu.VMEM((rows + NJ, N2), F32),
             pltpu.VMEM((rows, N2), BF),
             pltpu.SemaphoreType.DMA((n_hist + 1, signals // 16)),
             pltpu.SemaphoreType.DMA((NJ,)),
         ],
         cost_estimate=pl.CostEstimate(flops=n_out * 10**10, transcendentals=0, bytes_accessed=n_out * 10**7),
-        compiler_params=pltpu.CompilerParams(vmem_limit_bytes=56 * 1024 * 1024),
+        compiler_params=pltpu.CompilerParams(vmem_limit_bytes=58 * 1024 * 1024),
     )(mask, voltages, *parts, window, jnp.asarray(twiddle_table()), jnp.asarray(bin_table()))
 
 

time: 170 us -> 169 us (level)
  Pallas kernels: 51.2 us -> 39 us
  waiting for transfers between devices: 80.2 us -> 86.3 us
  starting transfers between devices: 31.6 us -> 37 us
    pallas_call x2, Pallas kernels: 36.6 us -> 24.4 us  [spectra_call(): pl.pallas_call(lambda *refs: fft_kernel(n_out, len(parts), slots, taps_a,...]
    all_to_all x1, waiting for transfers between devices: 6.39 us -> 12.5 us  [per_device(): lax.all_to_all(first, ('ta', 'aa'), split_axis=0, concat_axis=0, tiled=True)]
    all_to_all x1, starting transfers between devices: 8.14 us -> 13.5 us  [per_device(): lax.all_to_all(second, ('ta', 'aa'), split_axis=0, concat_axis=0, tiled=T...]
  transfers between devices with their start and end apart: 7 -> 7, of which waited for: 4 -> 4; matrix products, arithmetic and copies ran while one was open for 0% -> 0% of each run, Pallas kernels for 25% -> 18%
where the time goes in v2:
time: 169 us; the launch traced here: 167 us
  waiting for transfers between devices  86.3 us (51%)
  Pallas kernels  39 us (23%)
  starting transfers between devices  37 us (22%)
  local copies, waits for them, and re-layouts  4.46 us (3%)
    all_to_all x1, waiting for transfers between devices, per_device(): lax.all_to_all(second, ('ta', 'aa'), split_axis=0, concat_axis=0, tiled=T...  48.5 us
    pallas_call x2, Pallas kernels, spectra_call(): pl.pallas_call(lambda *refs: fft_kernel(n_out, len(parts), slots, taps_a,...  24.4 us
    ppermute x1, waiting for transfers between devices, per_device(): got = lax.ppermute(send, 'aa', [(0, 1), (1, 0)])  19.4 us
    all_to_all x1, starting transfers between devices, per_device(): lax.all_to_all(first, ('ta', 'aa'), split_axis=0, concat_axis=0, tiled=True)  15.5 us
    all_to_all x1, starting transfers between devices, per_device(): lax.all_to_all(second, ('ta', 'aa'), split_axis=0, concat_axis=0, tiled=T...  13.5 us
    all_to_all x1, waiting for transfers between devices, per_device(): lax.all_to_all(first, ('ta', 'aa'), split_axis=0, concat_axis=0, tiled=True)  12.5 us
    pallas_call x2, Pallas kernels, cut(): pl.pallas_call(lambda *refs: cut_kernel(plan, *refs), out_shape=[jax.Shap...  7.2 us
    ppermute x1, waiting for transfers between devices, per_device(): prev_a = lax.ppermute(to_r, 'ta', to_right)  5.8 us
  transfers between devices with their start and end apart: 7, of which 4 were waited for; matrix products, arithmetic and copies ran while one was open for 0% of the time, Pallas kernels for 18%

profile of v2, /device:TPU:64, one launch (start us, length us, event | category | flops | bytes accessed | tf_op | source)
XLA Modules:
  0.0 167.0 jit_solution(4928675619313680258)
XLA Ops:
  0.0 2.9 %shard_map.64 = (bf16[64,8192]{1,0:T(8,128)(2,1)}, bf16[64,8192]{1,0:T(8,128)(2,1)}) custom-call(bf16[128,24576]{1,0:T(8,128)(2,1)} %refs_1_.3), custom_call_target="tpu_custom_call" | custom-call | flops 1000000000 | bytes 10000000 | tf_op jit(solution)/shard_map/pallas_call | solution.py:449
  2.9 1.9 %collective-permute-start = (bf16[64,8192]{1,0:T(8,128)(2,1)}, bf16[64,8192]{1,0:T(8,128)(2,1)S(1)}, u32[]{:S(2)}, u32[]{:S(2)}) collective-permute-start(bf16[64,8192]{1,0:T(8,128)(2,1)} %get-tuple-element.11), channel_id=1, source_target_pairs={{0,2},{2,4},{4,6},{6,8},{8,10},{10,12},{12,14},{14,16},{16,18},{18... | collective-permute-start | bytes 3145736 | tf_op jit(solution)/shard_map/ppermute | solution.py:469
  4.9 1.8 %collective-permute-start.1 = (bf16[64,8192]{1,0:T(8,128)(2,1)}, bf16[64,8192]{1,0:T(8,128)(2,1)}, u32[]{:S(2)}, u32[]{:S(2)}) collective-permute-start(bf16[64,8192]{1,0:T(8,128)(2,1)} %get-tuple-element.12), channel_id=1, source_target_pairs={{0,254},{2,0},{4,2},{6,4},{8,6},{10,8},{12,10},{14,12},{16,14},{18... | collective-permute-start | bytes 3145736 | tf_op jit(solution)/shard_map/ppermute | solution.py:470
  6.7 4.3 %shard_map.67 = (bf16[128,8192]{1,0:T(8,128)(2,1)}, bf16[128,8192]{1,0:T(8,128)(2,1)}) custom-call(bf16[128,24576]{1,0:T(8,128)(2,1)} %refs_1_.3), custom_call_target="tpu_custom_call" | custom-call | flops 1000000000 | bytes 10000000 | tf_op jit(solution)/shard_map/pallas_call | solution.py:449
  11.0 0.1 collective-permute-start.2
  11.1 2.4 %collective-permute-start.3 = (bf16[128,8192]{1,0:T(8,128)(2,1)}, bf16[128,8192]{1,0:T(8,128)(2,1)}, u32[]{:S(2)}, u32[]{:S(2)}) collective-permute-start(bf16[128,8192]{1,0:T(8,128)(2,1)} %get-tuple-element.14), channel_id=1, source_target_pairs={{0,2},{2,4},{4,6},{6,8},{8,10},{10,12},{12,14},{14,16},{16,18},{18... | collective-permute-start | bytes 6291464 | tf_op jit(solution)/shard_map/ppermute | solution.py:473
  13.5 5.8 %collective-permute-done.refs_2_ = bf16[64,8192]{1,0:T(8,128)(2,1)S(1)} collective-permute-done((bf16[64,8192]{1,0:T(8,128)(2,1)}, bf16[64,8192]{1,0:T(8,128)(2,1)S(1)}, u32[]{:S(2)}, u32[]{:S(2)}) %collective-permute-start) | collective-permute-done | bytes 1048608 | tf_op jit(solution)/shard_map/ppermute | solution.py:469
  19.3 0.0 collective-permute-done.1.refs_3_
  19.3 1.0 copy-done.3
  20.3 9.4 %shard_map.65 = bf16[4096,128]{1,0:T(8,128)(2,1)} custom-call(s32[1]{0:T(128)} %bitcast.1.refs_0_, bf16[128,24576]{1,0:T(8,128)(2,1)} %refs_1_.3, bf16[64,8192]{1,0:T(8,128)(2,1)} %copy-done.3, bf16[64,8192]{1,0:T(8,128)(2,1)} %collective-permute-done.1.refs_3_, f32[4,8192]{1,0:T(4,128)} %refs_6_.2, f32[33,2,128]{2,1,0:T(2,128)} %constant.14.clone.refs_5_.refs_7_, ...), custom_call_target="tpu_custom_call" | custom-call | flops 10000000000 | bytes 10000000 | tf_op jit(solution)/shard_map/pallas_call | solution.py:258
  29.7 15.5 %all-to-all-start = ((bf16[256,16,128]{2,1,0:T(8,128)(2,1)}), bf16[256,16,128]{2,1,0:T(8,128)(2,1)S(1)}, u32[]{:S(2)}, u32[]{:S(2)}) async-start(bf16[256,16,128]{2,1,0:T(8,128)(2,1)} %bitcast.9), calls=%async_computation | async-start | bytes 2097152 | tf_op jit(solution)/shard_map/all_to_all | solution.py:478
  45.2 0.0 collective-permute-done.2.refs_4_
  45.2 1.3 copy-done.2
  46.5 15.0 %shard_map.68 = bf16[8192,128]{1,0:T(8,128)(2,1)} custom-call(s32[1]{0:T(128)} %bitcast.1.refs_0_, bf16[128,24576]{1,0:T(8,128)(2,1)} %refs_1_.3, bf16[64,8192]{1,0:T(8,128)(2,1)} %copy-done.3, bf16[64,8192]{1,0:T(8,128)(2,1)} %collective-permute-done.1.refs_3_, bf16[128,8192]{1,0:T(8,128)(2,1)} %copy-done.2, ...), custom_call_target="tpu_custom_call" | custom-call | flops 20000000000 | bytes 20000000 | tf_op jit(solution)/shard_map/pallas_call | solution.py:258
  61.5 12.5 %all-to-all-done = bf16[256,16,128]{2,1,0:T(8,128)(2,1)S(1)} async-done(((bf16[256,16,128]{2,1,0:T(8,128)(2,1)}), bf16[256,16,128]{2,1,0:T(8,128)(2,1)S(1)}, u32[]{:S(2)}, u32[]{:S(2)}) %all-to-all-start) | async-done | bytes 1048608 | tf_op jit(solution)/shard_map/all_to_all | solution.py:478
  74.0 13.5 %all-to-all-start.1 = ((bf16[256,32,128]{2,1,0:T(8,128)(2,1)}), bf16[256,32,128]{2,1,0:T(8,128)(2,1)S(1)}, u32[]{:S(2)}, u32[]{:S(2)}) async-start(bf16[256,32,128]{2,1,0:T(8,128)(2,1)} %bitcast.8), calls=%async_computation.1 | async-start | bytes 4194304 | tf_op jit(solution)/shard_map/all_to_all | solution.py:482
  87.5 1.1 shard_map.66.first_ref
  88.6 1.0 copy-done
  89.6 48.5 %all-to-all-done.1 = bf16[256,32,128]{2,1,0:T(8,128)(2,1)S(1)} async-done(((bf16[256,32,128]{2,1,0:T(8,128)(2,1)}), bf16[256,32,128]{2,1,0:T(8,128)(2,1)S(1)}, u32[]{:S(2)}, u32[]{:S(2)}) %all-to-all-start.1) | async-done | bytes 2097184 | tf_op jit(solution)/shard_map/all_to_all | solution.py:482
  138.1 1.2 copy-done.1
  139.3 4.8 %shard_map.69 = (f32[16,128,512]{2,1,0:T(8,128)}, bf16[8,128,384]{2,1,0:T(8,128)(2,1)S(1)}) custom-call(s32[1]{0:T(128)} %bitcast.own_ref, bf16[8,256,256]{2,1,0:T(8,128)(2,1)S(1)} %copy-done.1, bf16[8192,128]{1,0:T(8,128)(2,1)S(1)} %bitcast.6), custom_call_target="tpu_custom_call" | custom-call | flops 5000000000 | bytes 10000000 | tf_op jit(solution)/shard_map/pallas_call | solution.py:369
  144.1 1.7 %collective-permute-start.4 = (bf16[8,128,384]{2,1,0:T(8,128)(2,1)S(1)}, bf16[8,128,384]{2,1,0:T(8,128)(2,1)S(1)}, u32[]{:S(2)}, u32[]{:S(2)}) collective-permute-start(bf16[8,128,384]{2,1,0:T(8,128)(2,1)S(1)} %get-tuple-element.16), channel_id=1, source_target_pairs={{0,1},{1,0},{2,3},{3,2},{4,5},{5,4},{6,7},{7,6},{8,9},{9,8},{10,11... | collective-permute-start | bytes 2359304 | tf_op jit(solution)/shard_map/ppermute | solution.py:485
  145.8 19.4 %collective-permute-done.4.got_ref = bf16[8,128,384]{2,1,0:T(8,128)(2,1)S(1)} collective-permute-done((bf16[8,128,384]{2,1,0:T(8,128)(2,1)S(1)}, bf16[8,128,384]{2,1,0:T(8,128)(2,1)S(1)}, u32[]{:S(2)}, u32[]{:S(2)}) %collective-permute-start.4) | collective-permute-done | bytes 786464 | tf_op jit(solution)/shard_map/ppermute | solution.py:485
  165.3 1.6 shard_map.70
  (5 shorter events, 0.0 us)
Async XLA Ops:
  2.9 16.3 %collective-permute-start = (bf16[64,8192]{1,0:T(8,128)(2,1)}, bf16[64,8192]{1,0:T(8,128)(2,1)S(1)}, u32[]{:S(2)}, u32[]{:S(2)}) collective-permute-start(bf16[64,8192]{1,0:T(8,128)(2,1)} %get-tuple-element.11), channel_id=1, source_target_pairs={{0,2},{2,4},{4,6},{6,8},{8,10},{10,12},{12,14},{14,16},{16,18},{18... | collective-permute-start | bytes 3145736 | tf_op jit(solution)/shard_map/ppermute | solution.py:469
  4.9 14.4 %collective-permute-start.1 = (bf16[64,8192]{1,0:T(8,128)(2,1)}, bf16[64,8192]{1,0:T(8,128)(2,1)}, u32[]{:S(2)}, u32[]{:S(2)}) collective-permute-start(bf16[64,8192]{1,0:T(8,128)(2,1)} %get-tuple-element.12), channel_id=1, source_target_pairs={{0,254},{2,0},{4,2},{6,4},{8,6},{10,8},{12,10},{14,12},{16,14},{18... | collective-permute-start | bytes 3145736 | tf_op jit(solution)/shard_map/ppermute | solution.py:470
  11.0 34.2 %collective-permute-start.2 = (bf16[128,8192]{1,0:T(8,128)(2,1)}, bf16[128,8192]{1,0:T(8,128)(2,1)S(1)}, u32[]{:S(2)}, u32[]{:S(2)}) collective-permute-start(bf16[128,8192]{1,0:T(8,128)(2,1)} %get-tuple-element.13), channel_id=1, source_target_pairs={{0,254},{2,0},{4,2},{6,4},{8,6},{10,8},{12,10},{14,12},{16,14},{18... | collective-permute-start | bytes 6291464 | tf_op jit(solution)/shard_map/ppermute | solution.py:474
  11.1 34.1 %collective-permute-start.3 = (bf16[128,8192]{1,0:T(8,128)(2,1)}, bf16[128,8192]{1,0:T(8,128)(2,1)}, u32[]{:S(2)}, u32[]{:S(2)}) collective-permute-start(bf16[128,8192]{1,0:T(8,128)(2,1)} %get-tuple-element.14), channel_id=1, source_target_pairs={{0,2},{2,4},{4,6},{6,8},{8,10},{10,12},{12,14},{14,16},{16,18},{18... | collective-permute-start | bytes 6291464 | tf_op jit(solution)/shard_map/ppermute | solution.py:473
  19.3 1.0 copy-start.3
  29.7 44.3 %all-to-all-start = ((bf16[256,16,128]{2,1,0:T(8,128)(2,1)}), bf16[256,16,128]{2,1,0:T(8,128)(2,1)S(1)}, u32[]{:S(2)}, u32[]{:S(2)}) async-start(bf16[256,16,128]{2,1,0:T(8,128)(2,1)} %bitcast.9), calls=%async_computation | async-start | bytes 2097152 | tf_op jit(solution)/shard_map/all_to_all | solution.py:478
  45.2 1.3 copy-start.2
  74.0 64.1 %all-to-all-start.1 = ((bf16[256,32,128]{2,1,0:T(8,128)(2,1)}), bf16[256,32,128]{2,1,0:T(8,128)(2,1)S(1)}, u32[]{:S(2)}, u32[]{:S(2)}) async-start(bf16[256,32,128]{2,1,0:T(8,128)(2,1)} %bitcast.8), calls=%async_computation.1 | async-start | bytes 4194304 | tf_op jit(solution)/shard_map/all_to_all | solution.py:482
  88.6 1.0 copy-start
  138.1 1.2 copy-start.1
  144.1 21.2 %collective-permute-start.4 = (bf16[8,128,384]{2,1,0:T(8,128)(2,1)S(1)}, bf16[8,128,384]{2,1,0:T(8,128)(2,1)S(1)}, u32[]{:S(2)}, u32[]{:S(2)}) collective-permute-start(bf16[8,128,384]{2,1,0:T(8,128)(2,1)S(1)} %get-tuple-element.16), channel_id=1, source_target_pairs={{0,1},{1,0},{2,3},{3,2},{4,5},{5,4},{6,7},{7,6},{8,9},{9,8},{10,11... | collective-permute-start | bytes 2359304 | tf_op jit(solution)/shard_map/ppermute | solution.py:485

commit v3 on v2

--- a/solution.py
+++ b/solution.py
@@ -271,7 +271,7 @@
             pltpu.SemaphoreType.DMA((NJ,)),
         ],
         cost_estimate=pl.CostEstimate(flops=n_out * 10**10, transcendentals=0, bytes_accessed=n_out * 10**7),
-        compiler_params=pltpu.CompilerParams(vmem_limit_bytes=58 * 1024 * 1024),
+        compiler_params=pltpu.CompilerParams(vmem_limit_bytes=127 * 512 * 1024),
     )(mask, voltages, *parts, window, jnp.asarray(twiddle_table()), jnp.asarray(bin_table()))
 
 
@@ -286,7 +286,7 @@
                 wide[src, pl.ds(part * N2 + t, 8, stride=LAP), :] = tile[part * 8 : part * 8 + 8]
         return carry
 
-    lax.fori_loop(0, N2, body, 0)
+    lax.fori_loop(0, N2, body, 0, unroll=4)
     for ch in range(8):
         for src in range(2):
             out_ref[ch, :, src * N2 : (src + 1) * N2] = wide[src, ch * LAP : ch * LAP + 2 * N2, :].astype(BF)
@@ -322,7 +322,7 @@
                     wide[f, src, pl.ds(part * N2 + t, 8, stride=LAP), :] = tile[part * 8 : part * 8 + 8]
         return carry
 
-    lax.fori_loop(0, N2, body, 0)
+    lax.fori_loop(0, N2, body, 0, unroll=4)
 
     first = own == 0
     mine = pl.ds(pl.multiple_of(own * N2, N2), N2)
@@ -453,7 +453,7 @@
         out_specs=[pl.BlockSpec(memory_space=pltpu.VMEM)] * len(plan),
         scratch_shapes=[pltpu.SemaphoreType.DMA((sum(sizes) // 16,))],
         cost_estimate=pl.CostEstimate(flops=10**9, transcendentals=0, bytes_accessed=10**7),
-        compiler_params=pltpu.CompilerParams(vmem_limit_bytes=60 * 1024 * 1024),
+        compiler_params=pltpu.CompilerParams(vmem_limit_bytes=127 * 512 * 1024),
     )(voltages)
 
 

time: 169 us -> 166 us (0.982)
  local copies, waits for them, and re-layouts: 4.46 us -> 0 us
    unnamed x8 -> x0, local copies, waits for them, and re-layouts: 4.46 us -> none
    all_to_all x1, starting transfers between devices: 15.5 us -> 17.4 us  [per_device(): lax.all_to_all(first, ('ta', 'aa'), split_axis=0, concat_axis=0, tiled=True)]
  transfers between devices with their start and end apart: 7 -> 7, of which waited for: 4 -> 4; matrix products, arithmetic and copies ran while one was open for 0% -> 0% of each run, Pallas kernels for 18% -> 19%
where the time goes in v3:
time: 166 us; the launch traced here: 164 us
  waiting for transfers between devices  87 us (52%)
  Pallas kernels  39.1 us (24%)
  starting transfers between devices  37.7 us (23%)
    all_to_all x1, waiting for transfers between devices, per_device(): lax.all_to_all(second, ('ta', 'aa'), split_axis=0, concat_axis=0, tiled=T...  48.8 us
    pallas_call x2, Pallas kernels, spectra_call(): pl.pallas_call(lambda *refs: fft_kernel(n_out, len(parts), slots, taps_a,...  24.3 us
    ppermute x1, waiting for transfers between devices, per_device(): got = lax.ppermute(send, 'aa', [(0, 1), (1, 0)])  19.4 us
    all_to_all x1, starting transfers between devices, per_device(): lax.all_to_all(first, ('ta', 'aa'), split_axis=0, concat_axis=0, tiled=True)  17.4 us
    all_to_all x1, waiting for transfers between devices, per_device(): lax.all_to_all(first, ('ta', 'aa'), split_axis=0, concat_axis=0, tiled=True)  12.9 us
    all_to_all x1, starting transfers between devices, per_device(): lax.all_to_all(second, ('ta', 'aa'), split_axis=0, concat_axis=0, tiled=T...  12.4 us
    pallas_call x2, Pallas kernels, cut(): pl.pallas_call(lambda *refs: cut_kernel(plan, *refs), out_shape=[jax.Shap...  7.22 us
    ppermute x1, waiting for transfers between devices, per_device(): prev_a = lax.ppermute(to_r, 'ta', to_right)  5.9 us
  transfers between devices with their start and end apart: 7, of which 4 were waited for; matrix products, arithmetic and copies ran while one was open for 0% of the time, Pallas kernels for 19%

profile of v3, /device:TPU:64, one launch (start us, length us, event | category | flops | bytes accessed | tf_op | source)
XLA Modules:
  0.0 164.1 jit_solution(15625164791192009741)
XLA Ops:
  0.0 2.9 %shard_map.64 = (bf16[64,8192]{1,0:T(8,128)(2,1)}, bf16[64,8192]{1,0:T(8,128)(2,1)}) custom-call(bf16[128,24576]{1,0:T(8,128)(2,1)} %refs_1_.3), custom_call_target="tpu_custom_call" | custom-call | flops 1000000000 | bytes 10000000 | tf_op jit(solution)/shard_map/pallas_call | solution.py:449
  2.9 1.9 %collective-permute-start = (bf16[64,8192]{1,0:T(8,128)(2,1)}, bf16[64,8192]{1,0:T(8,128)(2,1)}, u32[]{:S(2)}, u32[]{:S(2)}) collective-permute-start(bf16[64,8192]{1,0:T(8,128)(2,1)} %get-tuple-element.11), channel_id=1, source_target_pairs={{0,2},{2,4},{4,6},{6,8},{8,10},{10,12},{12,14},{14,16},{16,18},{18... | collective-permute-start | bytes 3145736 | tf_op jit(solution)/shard_map/ppermute | solution.py:469
  4.9 1.8 %collective-permute-start.1 = (bf16[64,8192]{1,0:T(8,128)(2,1)}, bf16[64,8192]{1,0:T(8,128)(2,1)}, u32[]{:S(2)}, u32[]{:S(2)}) collective-permute-start(bf16[64,8192]{1,0:T(8,128)(2,1)} %get-tuple-element.12), channel_id=1, source_target_pairs={{0,254},{2,0},{4,2},{6,4},{8,6},{10,8},{12,10},{14,12},{16,14},{18... | collective-permute-start | bytes 3145736 | tf_op jit(solution)/shard_map/ppermute | solution.py:470
  6.7 4.3 %shard_map.67 = (bf16[128,8192]{1,0:T(8,128)(2,1)}, bf16[128,8192]{1,0:T(8,128)(2,1)}) custom-call(bf16[128,24576]{1,0:T(8,128)(2,1)} %refs_1_.3), custom_call_target="tpu_custom_call" | custom-call | flops 1000000000 | bytes 10000000 | tf_op jit(solution)/shard_map/pallas_call | solution.py:449
  11.0 0.1 collective-permute-start.2
  11.1 2.4 %collective-permute-start.3 = (bf16[128,8192]{1,0:T(8,128)(2,1)}, bf16[128,8192]{1,0:T(8,128)(2,1)}, u32[]{:S(2)}, u32[]{:S(2)}) collective-permute-start(bf16[128,8192]{1,0:T(8,128)(2,1)} %get-tuple-element.14), channel_id=1, source_target_pairs={{0,2},{2,4},{4,6},{6,8},{8,10},{10,12},{12,14},{14,16},{16,18},{18... | collective-permute-start | bytes 6291464 | tf_op jit(solution)/shard_map/ppermute | solution.py:473
  13.5 5.9 %collective-permute-done.refs_2_ = bf16[64,8192]{1,0:T(8,128)(2,1)} collective-permute-done((bf16[64,8192]{1,0:T(8,128)(2,1)}, bf16[64,8192]{1,0:T(8,128)(2,1)}, u32[]{:S(2)}, u32[]{:S(2)}) %collective-permute-start) | collective-permute-done | bytes 1048608 | tf_op jit(solution)/shard_map/ppermute | solution.py:469
  19.4 0.0 collective-permute-done.1.refs_3_
  19.4 9.4 %shard_map.65 = bf16[4096,128]{1,0:T(8,128)(2,1)} custom-call(s32[1]{0:T(128)} %bitcast.1.refs_0_, bf16[128,24576]{1,0:T(8,128)(2,1)} %refs_1_.3, bf16[64,8192]{1,0:T(8,128)(2,1)} %collective-permute-done.refs_2_, bf16[64,8192]{1,0:T(8,128)(2,1)} %collective-permute-done.1.refs_3_, f32[4,8192]{1,0:T(4,128)} %refs_6_.2, ...), custom_call_target="tpu_custom_call" | custom-call | flops 10000000000 | bytes 10000000 | tf_op jit(solution)/shard_map/pallas_call | solution.py:258
  28.7 17.4 %all-to-all-start = ((bf16[256,16,128]{2,1,0:T(8,128)(2,1)}), bf16[256,16,128]{2,1,0:T(8,128)(2,1)}, u32[]{:S(2)}, u32[]{:S(2)}) async-start(bf16[256,16,128]{2,1,0:T(8,128)(2,1)} %bitcast.8), calls=%async_computation | async-start | bytes 2097152 | tf_op jit(solution)/shard_map/all_to_all | solution.py:478
  46.1 0.0 collective-permute-done.2.refs_4_
  46.1 0.0 collective-permute-done.3.refs_5_
  46.1 15.0 %shard_map.68 = bf16[8192,128]{1,0:T(8,128)(2,1)} custom-call(s32[1]{0:T(128)} %bitcast.1.refs_0_, bf16[128,24576]{1,0:T(8,128)(2,1)} %refs_1_.3, bf16[64,8192]{1,0:T(8,128)(2,1)} %collective-permute-done.refs_2_, bf16[64,8192]{1,0:T(8,128)(2,1)} %collective-permute-done.1.refs_3_, bf16[128,8192]{1,0:T(8,128)(2,1)} %collective-permute-done.2.refs_4_, ...), custom_call_target="tpu_custom_call" | custom-call | flops 20000000000 | bytes 20000000 | tf_op jit(solution)/shard_map/pallas_call | solution.py:258
  61.1 12.9 %all-to-all-done = bf16[256,16,128]{2,1,0:T(8,128)(2,1)} async-done(((bf16[256,16,128]{2,1,0:T(8,128)(2,1)}), bf16[256,16,128]{2,1,0:T(8,128)(2,1)}, u32[]{:S(2)}, u32[]{:S(2)}) %all-to-all-start) | async-done | bytes 1048608 | tf_op jit(solution)/shard_map/all_to_all | solution.py:478
  74.0 12.4 %all-to-all-start.1 = ((bf16[256,32,128]{2,1,0:T(8,128)(2,1)}), bf16[256,32,128]{2,1,0:T(8,128)(2,1)S(1)}, u32[]{:S(2)}, u32[]{:S(2)}) async-start(bf16[256,32,128]{2,1,0:T(8,128)(2,1)} %bitcast.7), calls=%async_computation.1 | async-start | bytes 4194304 | tf_op jit(solution)/shard_map/all_to_all | solution.py:482
  86.4 1.8 %shard_map.66.first_ref = bf16[8,256,256]{2,1,0:T(8,128)(2,1)S(1)} custom-call(bf16[4096,128]{1,0:T(8,128)(2,1)} %bitcast.3.in_ref), custom_call_target="tpu_custom_call" | custom-call | flops 2000000000 | bytes 1000000 | tf_op jit(solution)/shard_map/pallas_call | solution.py:297
  88.2 48.8 %all-to-all-done.1 = bf16[256,32,128]{2,1,0:T(8,128)(2,1)S(1)} async-done(((bf16[256,32,128]{2,1,0:T(8,128)(2,1)}), bf16[256,32,128]{2,1,0:T(8,128)(2,1)S(1)}, u32[]{:S(2)}, u32[]{:S(2)}) %all-to-all-start.1) | async-done | bytes 2097184 | tf_op jit(solution)/shard_map/all_to_all | solution.py:482
  137.0 4.2 %shard_map.69 = (f32[16,128,512]{2,1,0:T(8,128)}, bf16[8,128,384]{2,1,0:T(8,128)(2,1)S(1)}) custom-call(s32[1]{0:T(128)} %bitcast.own_ref, bf16[8,256,256]{2,1,0:T(8,128)(2,1)S(1)} %shard_map.66.first_ref, bf16[8192,128]{1,0:T(8,128)(2,1)S(1)} %bitcast.6), custom_call_target="tpu_custom_call" | custom-call | flops 5000000000 | bytes 10000000 | tf_op jit(solution)/shard_map/pallas_call | solution.py:369
  141.2 1.7 %collective-permute-start.4 = (bf16[8,128,384]{2,1,0:T(8,128)(2,1)S(1)}, bf16[8,128,384]{2,1,0:T(8,128)(2,1)S(1)}, u32[]{:S(2)}, u32[]{:S(2)}) collective-permute-start(bf16[8,128,384]{2,1,0:T(8,128)(2,1)S(1)} %get-tuple-element.16), channel_id=1, source_target_pairs={{0,1},{1,0},{2,3},{3,2},{4,5},{5,4},{6,7},{7,6},{8,9},{9,8},{10,11... | collective-permute-start | bytes 2359304 | tf_op jit(solution)/shard_map/ppermute | solution.py:485
  143.0 19.4 %collective-permute-done.4.got_ref = bf16[8,128,384]{2,1,0:T(8,128)(2,1)S(1)} collective-permute-done((bf16[8,128,384]{2,1,0:T(8,128)(2,1)S(1)}, bf16[8,128,384]{2,1,0:T(8,128)(2,1)S(1)}, u32[]{:S(2)}, u32[]{:S(2)}) %collective-permute-start.4) | collective-permute-done | bytes 786464 | tf_op jit(solution)/shard_map/ppermute | solution.py:485
  162.4 1.6 shard_map.70
Async XLA Ops:
  2.9 16.4 %collective-permute-start = (bf16[64,8192]{1,0:T(8,128)(2,1)}, bf16[64,8192]{1,0:T(8,128)(2,1)}, u32[]{:S(2)}, u32[]{:S(2)}) collective-permute-start(bf16[64,8192]{1,0:T(8,128)(2,1)} %get-tuple-element.11), channel_id=1, source_target_pairs={{0,2},{2,4},{4,6},{6,8},{8,10},{10,12},{12,14},{14,16},{16,18},{18... | collective-permute-start | bytes 3145736 | tf_op jit(solution)/shard_map/ppermute | solution.py:469
  4.9 14.5 %collective-permute-start.1 = (bf16[64,8192]{1,0:T(8,128)(2,1)}, bf16[64,8192]{1,0:T(8,128)(2,1)}, u32[]{:S(2)}, u32[]{:S(2)}) collective-permute-start(bf16[64,8192]{1,0:T(8,128)(2,1)} %get-tuple-element.12), channel_id=1, source_target_pairs={{0,254},{2,0},{4,2},{6,4},{8,6},{10,8},{12,10},{14,12},{16,14},{18... | collective-permute-start | bytes 3145736 | tf_op jit(solution)/shard_map/ppermute | solution.py:470
  11.0 35.1 %collective-permute-start.2 = (bf16[128,8192]{1,0:T(8,128)(2,1)}, bf16[128,8192]{1,0:T(8,128)(2,1)}, u32[]{:S(2)}, u32[]{:S(2)}) collective-permute-start(bf16[128,8192]{1,0:T(8,128)(2,1)} %get-tuple-element.13), channel_id=1, source_target_pairs={{0,254},{2,0},{4,2},{6,4},{8,6},{10,8},{12,10},{14,12},{16,14},{18... | collective-permute-start | bytes 6291464 | tf_op jit(solution)/shard_map/ppermute | solution.py:474
  11.1 35.1 %collective-permute-start.3 = (bf16[128,8192]{1,0:T(8,128)(2,1)}, bf16[128,8192]{1,0:T(8,128)(2,1)}, u32[]{:S(2)}, u32[]{:S(2)}) collective-permute-start(bf16[128,8192]{1,0:T(8,128)(2,1)} %get-tuple-element.14), channel_id=1, source_target_pairs={{0,2},{2,4},{4,6},{6,8},{8,10},{10,12},{12,14},{14,16},{16,18},{18... | collective-permute-start | bytes 6291464 | tf_op jit(solution)/shard_map/ppermute | solution.py:473
  28.7 45.3 %all-to-all-start = ((bf16[256,16,128]{2,1,0:T(8,128)(2,1)}), bf16[256,16,128]{2,1,0:T(8,128)(2,1)}, u32[]{:S(2)}, u32[]{:S(2)}) async-start(bf16[256,16,128]{2,1,0:T(8,128)(2,1)} %bitcast.8), calls=%async_computation | async-start | bytes 2097152 | tf_op jit(solution)/shard_map/all_to_all | solution.py:478
  74.0 63.0 %all-to-all-start.1 = ((bf16[256,32,128]{2,1,0:T(8,128)(2,1)}), bf16[256,32,128]{2,1,0:T(8,128)(2,1)S(1)}, u32[]{:S(2)}, u32[]{:S(2)}) async-start(bf16[256,32,128]{2,1,0:T(8,128)(2,1)} %bitcast.7), calls=%async_computation.1 | async-start | bytes 4194304 | tf_op jit(solution)/shard_map/all_to_all | solution.py:482
  141.2 21.2 %collective-permute-start.4 = (bf16[8,128,384]{2,1,0:T(8,128)(2,1)S(1)}, bf16[8,128,384]{2,1,0:T(8,128)(2,1)S(1)}, u32[]{:S(2)}, u32[]{:S(2)}) collective-permute-start(bf16[8,128,384]{2,1,0:T(8,128)(2,1)S(1)} %get-tuple-element.16), channel_id=1, source_target_pairs={{0,1},{1,0},{2,3},{3,2},{4,5},{5,4},{6,7},{7,6},{8,9},{9,8},{10,11... | collective-permute-start | bytes 2359304 | tf_op jit(solution)/shard_map/ppermute | solution.py:485

commit v4 on v3

--- a/solution.py
+++ b/solution.py
@@ -428,19 +428,25 @@
 
 
 def cut_kernel(plan, v_hbm, *refs):
-    outs, sems = refs[: len(plan)], refs[len(plan)]
+    outs, (buf, in_sems, out_sems) = refs[: len(plan)], refs[len(plan) :]
     jobs = []
     for out, pieces in zip(outs, plan):
         at = 0
         for (start, stop), frame in pieces:
             for row in range(start, stop, 16):
+                i = len(jobs)
                 source = v_hbm.at[pl.ds(row, 16), pl.ds(frame * NFFT, NFFT)]
-                jobs.append(pltpu.make_async_copy(source, out.at[pl.ds(at, 16)], sems.at[len(jobs)]))
+                fetch = pltpu.make_async_copy(source, buf.at[i], in_sems.at[i])
+                put = pltpu.make_async_copy(buf.at[i], out.at[pl.ds(at, 16)], out_sems.at[i])
+                jobs.append((fetch, put))
                 at += 16
-    for job in jobs:
-        job.start()
-    for job in jobs:
-        job.wait()
+    for fetch, _ in jobs:
+        fetch.start()
+    for fetch, put in jobs:
+        fetch.wait()
+        put.start()
+    for _, put in jobs:
+        put.wait()
 
 
 def cut(voltages, plan):
@@ -450,8 +456,12 @@
         lambda *refs: cut_kernel(plan, *refs),
         out_shape=[jax.ShapeDtypeStruct((size, NFFT), BF) for size in sizes],
         in_specs=[hbm],
-        out_specs=[pl.BlockSpec(memory_space=pltpu.VMEM)] * len(plan),
-        scratch_shapes=[pltpu.SemaphoreType.DMA((sum(sizes) // 16,))],
+        out_specs=[hbm] * len(plan),
+        scratch_shapes=[
+            pltpu.VMEM((sum(sizes) // 16, 16, NFFT), BF),
+            pltpu.SemaphoreType.DMA((sum(sizes) // 16,)),
+            pltpu.SemaphoreType.DMA((sum(sizes) // 16,)),
+        ],
         cost_estimate=pl.CostEstimate(flops=10**9, transcendentals=0, bytes_accessed=10**7),
         compiler_params=pltpu.CompilerParams(vmem_limit_bytes=127 * 512 * 1024),
     )(voltages)

time: 166 us -> 166 us (level)
  transfers between devices with their start and end apart: 7 -> 7, of which waited for: 4 -> 4; matrix products, arithmetic and copies ran while one was open for 0% -> 0% of each run, Pallas kernels for 19% -> 18%
where the time goes in v4:
time: 166 us; the launch traced here: 164 us
  waiting for transfers between devices  87.5 us (53%)
  Pallas kernels  38.2 us (23%)
  starting transfers between devices  37.7 us (23%)
    all_to_all x1, waiting for transfers between devices, per_device(): lax.all_to_all(second, ('ta', 'aa'), split_axis=0, concat_axis=0, tiled=T...  48.8 us
    pallas_call x2, Pallas kernels, spectra_call(): pl.pallas_call(lambda *refs: fft_kernel(n_out, len(parts), slots, taps_a,...  24.3 us
    ppermute x1, waiting for transfers between devices, per_device(): got = lax.ppermute(send, 'aa', [(0, 1), (1, 0)])  19.4 us
    all_to_all x1, starting transfers between devices, per_device(): lax.all_to_all(first, ('ta', 'aa'), split_axis=0, concat_axis=0, tiled=True)  17.4 us
    all_to_all x1, waiting for transfers between devices, per_device(): lax.all_to_all(first, ('ta', 'aa'), split_axis=0, concat_axis=0, tiled=True)  12.9 us
    all_to_all x1, starting transfers between devices, per_device(): lax.all_to_all(second, ('ta', 'aa'), split_axis=0, concat_axis=0, tiled=T...  12.4 us
    ppermute x1, waiting for transfers between devices, per_device(): prev_a = lax.ppermute(to_r, 'ta', to_right)  6.35 us
    pallas_call x2, Pallas kernels, cut(): pl.pallas_call(lambda *refs: cut_kernel(plan, *refs), out_shape=[jax.Shap...  6.3 us
  transfers between devices with their start and end apart: 7, of which 4 were waited for; matrix products, arithmetic and copies ran while one was open for 0% of the time, Pallas kernels for 18%

profile of v4, /device:TPU:64, one launch (start us, length us, event | category | flops | bytes accessed | tf_op | source)
XLA Modules:
  0.0 163.6 jit_solution(13338918479292484141)
XLA Ops:
  0.0 2.5 %shard_map.64 = (bf16[64,8192]{1,0:T(8,128)(2,1)}, bf16[64,8192]{1,0:T(8,128)(2,1)}) custom-call(bf16[128,24576]{1,0:T(8,128)(2,1)} %refs_1_.3), custom_call_target="tpu_custom_call" | custom-call | flops 1000000000 | bytes 10000000 | tf_op jit(solution)/shard_map/pallas_call | solution.py:455
  2.5 1.9 %collective-permute-start = (bf16[64,8192]{1,0:T(8,128)(2,1)}, bf16[64,8192]{1,0:T(8,128)(2,1)}, u32[]{:S(2)}, u32[]{:S(2)}) collective-permute-start(bf16[64,8192]{1,0:T(8,128)(2,1)} %get-tuple-element.11), channel_id=1, source_target_pairs={{0,2},{2,4},{4,6},{6,8},{8,10},{10,12},{12,14},{14,16},{16,18},{18... | collective-permute-start | bytes 3145736 | tf_op jit(solution)/shard_map/ppermute | solution.py:479
  4.4 1.8 %collective-permute-start.1 = (bf16[64,8192]{1,0:T(8,128)(2,1)}, bf16[64,8192]{1,0:T(8,128)(2,1)}, u32[]{:S(2)}, u32[]{:S(2)}) collective-permute-start(bf16[64,8192]{1,0:T(8,128)(2,1)} %get-tuple-element.12), channel_id=1, source_target_pairs={{0,254},{2,0},{4,2},{6,4},{8,6},{10,8},{12,10},{14,12},{16,14},{18... | collective-permute-start | bytes 3145736 | tf_op jit(solution)/shard_map/ppermute | solution.py:480
  6.2 3.8 %shard_map.67 = (bf16[128,8192]{1,0:T(8,128)(2,1)}, bf16[128,8192]{1,0:T(8,128)(2,1)}) custom-call(bf16[128,24576]{1,0:T(8,128)(2,1)} %refs_1_.3), custom_call_target="tpu_custom_call" | custom-call | flops 1000000000 | bytes 10000000 | tf_op jit(solution)/shard_map/pallas_call | solution.py:455
  10.1 0.1 collective-permute-start.2
  10.2 2.4 %collective-permute-start.3 = (bf16[128,8192]{1,0:T(8,128)(2,1)}, bf16[128,8192]{1,0:T(8,128)(2,1)}, u32[]{:S(2)}, u32[]{:S(2)}) collective-permute-start(bf16[128,8192]{1,0:T(8,128)(2,1)} %get-tuple-element.14), channel_id=1, source_target_pairs={{0,2},{2,4},{4,6},{6,8},{8,10},{10,12},{12,14},{14,16},{16,18},{18... | collective-permute-start | bytes 6291464 | tf_op jit(solution)/shard_map/ppermute | solution.py:483
  12.6 6.3 %collective-permute-done.refs_2_ = bf16[64,8192]{1,0:T(8,128)(2,1)} collective-permute-done((bf16[64,8192]{1,0:T(8,128)(2,1)}, bf16[64,8192]{1,0:T(8,128)(2,1)}, u32[]{:S(2)}, u32[]{:S(2)}) %collective-permute-start) | collective-permute-done | bytes 1048608 | tf_op jit(solution)/shard_map/ppermute | solution.py:479
  18.9 0.0 collective-permute-done.1.refs_3_
  18.9 9.4 %shard_map.65 = bf16[4096,128]{1,0:T(8,128)(2,1)} custom-call(s32[1]{0:T(128)} %bitcast.1.refs_0_, bf16[128,24576]{1,0:T(8,128)(2,1)} %refs_1_.3, bf16[64,8192]{1,0:T(8,128)(2,1)} %collective-permute-done.refs_2_, bf16[64,8192]{1,0:T(8,128)(2,1)} %collective-permute-done.1.refs_3_, f32[4,8192]{1,0:T(4,128)} %refs_6_.2, ...), custom_call_target="tpu_custom_call" | custom-call | flops 10000000000 | bytes 10000000 | tf_op jit(solution)/shard_map/pallas_call | solution.py:258
  28.3 17.4 %all-to-all-start = ((bf16[256,16,128]{2,1,0:T(8,128)(2,1)}), bf16[256,16,128]{2,1,0:T(8,128)(2,1)}, u32[]{:S(2)}, u32[]{:S(2)}) async-start(bf16[256,16,128]{2,1,0:T(8,128)(2,1)} %bitcast.8), calls=%async_computation | async-start | bytes 2097152 | tf_op jit(solution)/shard_map/all_to_all | solution.py:488
  45.6 0.0 collective-permute-done.2.refs_4_
  45.7 0.0 collective-permute-done.3.refs_5_
  45.7 15.0 %shard_map.68 = bf16[8192,128]{1,0:T(8,128)(2,1)} custom-call(s32[1]{0:T(128)} %bitcast.1.refs_0_, bf16[128,24576]{1,0:T(8,128)(2,1)} %refs_1_.3, bf16[64,8192]{1,0:T(8,128)(2,1)} %collective-permute-done.refs_2_, bf16[64,8192]{1,0:T(8,128)(2,1)} %collective-permute-done.1.refs_3_, bf16[128,8192]{1,0:T(8,128)(2,1)} %collective-permute-done.2.refs_4_, ...), custom_call_target="tpu_custom_call" | custom-call | flops 20000000000 | bytes 20000000 | tf_op jit(solution)/shard_map/pallas_call | solution.py:258
  60.6 12.9 %all-to-all-done = bf16[256,16,128]{2,1,0:T(8,128)(2,1)} async-done(((bf16[256,16,128]{2,1,0:T(8,128)(2,1)}), bf16[256,16,128]{2,1,0:T(8,128)(2,1)}, u32[]{:S(2)}, u32[]{:S(2)}) %all-to-all-start) | async-done | bytes 1048608 | tf_op jit(solution)/shard_map/all_to_all | solution.py:488
  73.5 12.4 %all-to-all-start.1 = ((bf16[256,32,128]{2,1,0:T(8,128)(2,1)}), bf16[256,32,128]{2,1,0:T(8,128)(2,1)S(1)}, u32[]{:S(2)}, u32[]{:S(2)}) async-start(bf16[256,32,128]{2,1,0:T(8,128)(2,1)} %bitcast.7), calls=%async_computation.1 | async-start | bytes 4194304 | tf_op jit(solution)/shard_map/all_to_all | solution.py:492
  85.9 1.8 %shard_map.66.first_ref = bf16[8,256,256]{2,1,0:T(8,128)(2,1)S(1)} custom-call(bf16[4096,128]{1,0:T(8,128)(2,1)} %bitcast.3.in_ref), custom_call_target="tpu_custom_call" | custom-call | flops 2000000000 | bytes 1000000 | tf_op jit(solution)/shard_map/pallas_call | solution.py:297
  87.7 48.8 %all-to-all-done.1 = bf16[256,32,128]{2,1,0:T(8,128)(2,1)S(1)} async-done(((bf16[256,32,128]{2,1,0:T(8,128)(2,1)}), bf16[256,32,128]{2,1,0:T(8,128)(2,1)S(1)}, u32[]{:S(2)}, u32[]{:S(2)}) %all-to-all-start.1) | async-done | bytes 2097184 | tf_op jit(solution)/shard_map/all_to_all | solution.py:492
  136.5 4.2 %shard_map.69 = (f32[16,128,512]{2,1,0:T(8,128)}, bf16[8,128,384]{2,1,0:T(8,128)(2,1)S(1)}) custom-call(s32[1]{0:T(128)} %bitcast.own_ref, bf16[8,256,256]{2,1,0:T(8,128)(2,1)S(1)} %shard_map.66.first_ref, bf16[8192,128]{1,0:T(8,128)(2,1)S(1)} %bitcast.6), custom_call_target="tpu_custom_call" | custom-call | flops 5000000000 | bytes 10000000 | tf_op jit(solution)/shard_map/pallas_call | solution.py:369
  140.8 1.7 %collective-permute-start.4 = (bf16[8,128,384]{2,1,0:T(8,128)(2,1)S(1)}, bf16[8,128,384]{2,1,0:T(8,128)(2,1)S(1)}, u32[]{:S(2)}, u32[]{:S(2)}) collective-permute-start(bf16[8,128,384]{2,1,0:T(8,128)(2,1)S(1)} %get-tuple-element.16), channel_id=1, source_target_pairs={{0,1},{1,0},{2,3},{3,2},{4,5},{5,4},{6,7},{7,6},{8,9},{9,8},{10,11... | collective-permute-start | bytes 2359304 | tf_op jit(solution)/shard_map/ppermute | solution.py:495
  142.5 19.4 %collective-permute-done.4.got_ref = bf16[8,128,384]{2,1,0:T(8,128)(2,1)S(1)} collective-permute-done((bf16[8,128,384]{2,1,0:T(8,128)(2,1)S(1)}, bf16[8,128,384]{2,1,0:T(8,128)(2,1)S(1)}, u32[]{:S(2)}, u32[]{:S(2)}) %collective-permute-start.4) | collective-permute-done | bytes 786464 | tf_op jit(solution)/shard_map/ppermute | solution.py:495
  161.9 1.6 shard_map.70
Async XLA Ops:
  2.5 16.4 %collective-permute-start = (bf16[64,8192]{1,0:T(8,128)(2,1)}, bf16[64,8192]{1,0:T(8,128)(2,1)}, u32[]{:S(2)}, u32[]{:S(2)}) collective-permute-start(bf16[64,8192]{1,0:T(8,128)(2,1)} %get-tuple-element.11), channel_id=1, source_target_pairs={{0,2},{2,4},{4,6},{6,8},{8,10},{10,12},{12,14},{14,16},{16,18},{18... | collective-permute-start | bytes 3145736 | tf_op jit(solution)/shard_map/ppermute | solution.py:479
  4.4 14.5 %collective-permute-start.1 = (bf16[64,8192]{1,0:T(8,128)(2,1)}, bf16[64,8192]{1,0:T(8,128)(2,1)}, u32[]{:S(2)}, u32[]{:S(2)}) collective-permute-start(bf16[64,8192]{1,0:T(8,128)(2,1)} %get-tuple-element.12), channel_id=1, source_target_pairs={{0,254},{2,0},{4,2},{6,4},{8,6},{10,8},{12,10},{14,12},{16,14},{18... | collective-permute-start | bytes 3145736 | tf_op jit(solution)/shard_map/ppermute | solution.py:480
  10.1 35.6 %collective-permute-start.2 = (bf16[128,8192]{1,0:T(8,128)(2,1)}, bf16[128,8192]{1,0:T(8,128)(2,1)}, u32[]{:S(2)}, u32[]{:S(2)}) collective-permute-start(bf16[128,8192]{1,0:T(8,128)(2,1)} %get-tuple-element.13), channel_id=1, source_target_pairs={{0,254},{2,0},{4,2},{6,4},{8,6},{10,8},{12,10},{14,12},{16,14},{18... | collective-permute-start | bytes 6291464 | tf_op jit(solution)/shard_map/ppermute | solution.py:484
  10.2 35.5 %collective-permute-start.3 = (bf16[128,8192]{1,0:T(8,128)(2,1)}, bf16[128,8192]{1,0:T(8,128)(2,1)}, u32[]{:S(2)}, u32[]{:S(2)}) collective-permute-start(bf16[128,8192]{1,0:T(8,128)(2,1)} %get-tuple-element.14), channel_id=1, source_target_pairs={{0,2},{2,4},{4,6},{6,8},{8,10},{10,12},{12,14},{14,16},{16,18},{18... | collective-permute-start | bytes 6291464 | tf_op jit(solution)/shard_map/ppermute | solution.py:483
  28.3 45.3 %all-to-all-start = ((bf16[256,16,128]{2,1,0:T(8,128)(2,1)}), bf16[256,16,128]{2,1,0:T(8,128)(2,1)}, u32[]{:S(2)}, u32[]{:S(2)}) async-start(bf16[256,16,128]{2,1,0:T(8,128)(2,1)} %bitcast.8), calls=%async_computation | async-start | bytes 2097152 | tf_op jit(solution)/shard_map/all_to_all | solution.py:488
  73.5 63.0 %all-to-all-start.1 = ((bf16[256,32,128]{2,1,0:T(8,128)(2,1)}), bf16[256,32,128]{2,1,0:T(8,128)(2,1)S(1)}, u32[]{:S(2)}, u32[]{:S(2)}) async-start(bf16[256,32,128]{2,1,0:T(8,128)(2,1)} %bitcast.7), calls=%async_computation.1 | async-start | bytes 4194304 | tf_op jit(solution)/shard_map/all_to_all | solution.py:492
  140.8 21.2 %collective-permute-start.4 = (bf16[8,128,384]{2,1,0:T(8,128)(2,1)S(1)}, bf16[8,128,384]{2,1,0:T(8,128)(2,1)S(1)}, u32[]{:S(2)}, u32[]{:S(2)}) collective-permute-start(bf16[8,128,384]{2,1,0:T(8,128)(2,1)S(1)} %get-tuple-element.16), channel_id=1, source_target_pairs={{0,1},{1,0},{2,3},{3,2},{4,5},{5,4},{6,7},{7,6},{8,9},{9,8},{10,11... | collective-permute-start | bytes 2359304 | tf_op jit(solution)/shard_map/ppermute | solution.py:495

commit v5 on v4

--- a/solution.py
+++ b/solution.py
@@ -173,7 +173,7 @@
         copy_out(j).start()
         return carry
 
-    lax.fori_loop(0, NJ, narrow, 0)
+    lax.fori_loop(0, NJ, narrow, 0, unroll=4)
 
     def drain(j, carry):
         copy_out(j).wait()
@@ -286,7 +286,7 @@
                 wide[src, pl.ds(part * N2 + t, 8, stride=LAP), :] = tile[part * 8 : part * 8 + 8]
         return carry
 
-    lax.fori_loop(0, N2, body, 0, unroll=4)
+    lax.fori_loop(0, N2, body, 0, unroll=8)
     for ch in range(8):
         for src in range(2):
             out_ref[ch, :, src * N2 : (src + 1) * N2] = wide[src, ch * LAP : ch * LAP + 2 * N2, :].astype(BF)
@@ -322,7 +322,7 @@
                     wide[f, src, pl.ds(part * N2 + t, 8, stride=LAP), :] = tile[part * 8 : part * 8 + 8]
         return carry
 
-    lax.fori_loop(0, N2, body, 0, unroll=4)
+    lax.fori_loop(0, N2, body, 0, unroll=8)
 
     first = own == 0
     mine = pl.ds(pl.multiple_of(own * N2, N2), N2)

time: 166 us -> 166 us (level)
  no operation moved by 1% of the time
where the time goes in v5:
time: 166 us; the launch traced here: 164 us
  waiting for transfers between devices  87.6 us (53%)
  Pallas kernels  38.1 us (23%)
  starting transfers between devices  37.7 us (23%)
    all_to_all x1, waiting for transfers between devices, per_device(): lax.all_to_all(second, ('ta', 'aa'), split_axis=0, concat_axis=0, tiled=T...  48.9 us
    pallas_call x2, Pallas kernels, spectra_call(): pl.pallas_call(lambda *refs: fft_kernel(n_out, len(parts), slots, taps_a,...  24.3 us
    ppermute x1, waiting for transfers between devices, per_device(): got = lax.ppermute(send, 'aa', [(0, 1), (1, 0)])  19.4 us
    all_to_all x1, starting transfers between devices, per_device(): lax.all_to_all(first, ('ta', 'aa'), split_axis=0, concat_axis=0, tiled=True)  17.4 us
    all_to_all x1, waiting for transfers between devices, per_device(): lax.all_to_all(first, ('ta', 'aa'), split_axis=0, concat_axis=0, tiled=True)  12.9 us
    all_to_all x1, starting transfers between devices, per_device(): lax.all_to_all(second, ('ta', 'aa'), split_axis=0, concat_axis=0, tiled=T...  12.4 us
    ppermute x1, waiting for transfers between devices, per_device(): prev_a = lax.ppermute(to_r, 'ta', to_right)  6.35 us
    pallas_call x2, Pallas kernels, cut(): pl.pallas_call(lambda *refs: cut_kernel(plan, *refs), out_shape=[jax.Shap...  6.3 us
  transfers between devices with their start and end apart: 7, of which 4 were waited for; matrix products, arithmetic and copies ran while one was open for 0% of the time, Pallas kernels for 18%

profile of v5, /device:TPU:64, one launch (start us, length us, event | category | flops | bytes accessed | tf_op | source)
XLA Modules:
  0.0 163.6 jit_solution(5260646449890655492)
XLA Ops:
  0.0 2.5 %shard_map.64 = (bf16[64,8192]{1,0:T(8,128)(2,1)}, bf16[64,8192]{1,0:T(8,128)(2,1)}) custom-call(bf16[128,24576]{1,0:T(8,128)(2,1)} %refs_1_.3), custom_call_target="tpu_custom_call" | custom-call | flops 1000000000 | bytes 10000000 | tf_op jit(solution)/shard_map/pallas_call | solution.py:455
  2.5 1.9 %collective-permute-start = (bf16[64,8192]{1,0:T(8,128)(2,1)}, bf16[64,8192]{1,0:T(8,128)(2,1)}, u32[]{:S(2)}, u32[]{:S(2)}) collective-permute-start(bf16[64,8192]{1,0:T(8,128)(2,1)} %get-tuple-element.11), channel_id=1, source_target_pairs={{0,2},{2,4},{4,6},{6,8},{8,10},{10,12},{12,14},{14,16},{16,18},{18... | collective-permute-start | bytes 3145736 | tf_op jit(solution)/shard_map/ppermute | solution.py:479
  4.4 1.8 %collective-permute-start.1 = (bf16[64,8192]{1,0:T(8,128)(2,1)}, bf16[64,8192]{1,0:T(8,128)(2,1)}, u32[]{:S(2)}, u32[]{:S(2)}) collective-permute-start(bf16[64,8192]{1,0:T(8,128)(2,1)} %get-tuple-element.12), channel_id=1, source_target_pairs={{0,254},{2,0},{4,2},{6,4},{8,6},{10,8},{12,10},{14,12},{16,14},{18... | collective-permute-start | bytes 3145736 | tf_op jit(solution)/shard_map/ppermute | solution.py:480
  6.2 3.8 %shard_map.67 = (bf16[128,8192]{1,0:T(8,128)(2,1)}, bf16[128,8192]{1,0:T(8,128)(2,1)}) custom-call(bf16[128,24576]{1,0:T(8,128)(2,1)} %refs_1_.3), custom_call_target="tpu_custom_call" | custom-call | flops 1000000000 | bytes 10000000 | tf_op jit(solution)/shard_map/pallas_call | solution.py:455
  10.1 0.1 collective-permute-start.2
  10.2 2.4 %collective-permute-start.3 = (bf16[128,8192]{1,0:T(8,128)(2,1)}, bf16[128,8192]{1,0:T(8,128)(2,1)}, u32[]{:S(2)}, u32[]{:S(2)}) collective-permute-start(bf16[128,8192]{1,0:T(8,128)(2,1)} %get-tuple-element.14), channel_id=1, source_target_pairs={{0,2},{2,4},{4,6},{6,8},{8,10},{10,12},{12,14},{14,16},{16,18},{18... | collective-permute-start | bytes 6291464 | tf_op jit(solution)/shard_map/ppermute | solution.py:483
  12.6 6.3 %collective-permute-done.refs_2_ = bf16[64,8192]{1,0:T(8,128)(2,1)} collective-permute-done((bf16[64,8192]{1,0:T(8,128)(2,1)}, bf16[64,8192]{1,0:T(8,128)(2,1)}, u32[]{:S(2)}, u32[]{:S(2)}) %collective-permute-start) | collective-permute-done | bytes 1048608 | tf_op jit(solution)/shard_map/ppermute | solution.py:479
  18.9 0.0 collective-permute-done.1.refs_3_
  18.9 9.4 %shard_map.65 = bf16[4096,128]{1,0:T(8,128)(2,1)} custom-call(s32[1]{0:T(128)} %bitcast.1.refs_0_, bf16[128,24576]{1,0:T(8,128)(2,1)} %refs_1_.3, bf16[64,8192]{1,0:T(8,128)(2,1)} %collective-permute-done.refs_2_, bf16[64,8192]{1,0:T(8,128)(2,1)} %collective-permute-done.1.refs_3_, f32[4,8192]{1,0:T(4,128)} %refs_6_.2, ...), custom_call_target="tpu_custom_call" | custom-call | flops 10000000000 | bytes 10000000 | tf_op jit(solution)/shard_map/pallas_call | solution.py:258
  28.3 17.4 %all-to-all-start = ((bf16[256,16,128]{2,1,0:T(8,128)(2,1)}), bf16[256,16,128]{2,1,0:T(8,128)(2,1)}, u32[]{:S(2)}, u32[]{:S(2)}) async-start(bf16[256,16,128]{2,1,0:T(8,128)(2,1)} %bitcast.8), calls=%async_computation | async-start | bytes 2097152 | tf_op jit(solution)/shard_map/all_to_all | solution.py:488
  45.6 0.0 collective-permute-done.2.refs_4_
  45.7 0.0 collective-permute-done.3.refs_5_
  45.7 15.0 %shard_map.68 = bf16[8192,128]{1,0:T(8,128)(2,1)} custom-call(s32[1]{0:T(128)} %bitcast.1.refs_0_, bf16[128,24576]{1,0:T(8,128)(2,1)} %refs_1_.3, bf16[64,8192]{1,0:T(8,128)(2,1)} %collective-permute-done.refs_2_, bf16[64,8192]{1,0:T(8,128)(2,1)} %collective-permute-done.1.refs_3_, bf16[128,8192]{1,0:T(8,128)(2,1)} %collective-permute-done.2.refs_4_, ...), custom_call_target="tpu_custom_call" | custom-call | flops 20000000000 | bytes 20000000 | tf_op jit(solution)/shard_map/pallas_call | solution.py:258
  60.6 12.9 %all-to-all-done = bf16[256,16,128]{2,1,0:T(8,128)(2,1)} async-done(((bf16[256,16,128]{2,1,0:T(8,128)(2,1)}), bf16[256,16,128]{2,1,0:T(8,128)(2,1)}, u32[]{:S(2)}, u32[]{:S(2)}) %all-to-all-start) | async-done | bytes 1048608 | tf_op jit(solution)/shard_map/all_to_all | solution.py:488
  73.5 12.4 %all-to-all-start.1 = ((bf16[256,32,128]{2,1,0:T(8,128)(2,1)}), bf16[256,32,128]{2,1,0:T(8,128)(2,1)S(1)}, u32[]{:S(2)}, u32[]{:S(2)}) async-start(bf16[256,32,128]{2,1,0:T(8,128)(2,1)} %bitcast.7), calls=%async_computation.1 | async-start | bytes 4194304 | tf_op jit(solution)/shard_map/all_to_all | solution.py:492
  85.9 1.7 %shard_map.66.first_ref = bf16[8,256,256]{2,1,0:T(8,128)(2,1)S(1)} custom-call(bf16[4096,128]{1,0:T(8,128)(2,1)} %bitcast.3.in_ref), custom_call_target="tpu_custom_call" | custom-call | flops 2000000000 | bytes 1000000 | tf_op jit(solution)/shard_map/pallas_call | solution.py:297
  87.6 48.9 %all-to-all-done.1 = bf16[256,32,128]{2,1,0:T(8,128)(2,1)S(1)} async-done(((bf16[256,32,128]{2,1,0:T(8,128)(2,1)}), bf16[256,32,128]{2,1,0:T(8,128)(2,1)S(1)}, u32[]{:S(2)}, u32[]{:S(2)}) %all-to-all-start.1) | async-done | bytes 2097184 | tf_op jit(solution)/shard_map/all_to_all | solution.py:492
  136.5 4.2 %shard_map.69 = (f32[16,128,512]{2,1,0:T(8,128)}, bf16[8,128,384]{2,1,0:T(8,128)(2,1)S(1)}) custom-call(s32[1]{0:T(128)} %bitcast.own_ref, bf16[8,256,256]{2,1,0:T(8,128)(2,1)S(1)} %shard_map.66.first_ref, bf16[8192,128]{1,0:T(8,128)(2,1)S(1)} %bitcast.6), custom_call_target="tpu_custom_call" | custom-call | flops 5000000000 | bytes 10000000 | tf_op jit(solution)/shard_map/pallas_call | solution.py:369
  140.7 1.7 %collective-permute-start.4 = (bf16[8,128,384]{2,1,0:T(8,128)(2,1)S(1)}, bf16[8,128,384]{2,1,0:T(8,128)(2,1)S(1)}, u32[]{:S(2)}, u32[]{:S(2)}) collective-permute-start(bf16[8,128,384]{2,1,0:T(8,128)(2,1)S(1)} %get-tuple-element.16), channel_id=1, source_target_pairs={{0,1},{1,0},{2,3},{3,2},{4,5},{5,4},{6,7},{7,6},{8,9},{9,8},{10,11... | collective-permute-start | bytes 2359304 | tf_op jit(solution)/shard_map/ppermute | solution.py:495
  142.4 19.4 %collective-permute-done.4.got_ref = bf16[8,128,384]{2,1,0:T(8,128)(2,1)S(1)} collective-permute-done((bf16[8,128,384]{2,1,0:T(8,128)(2,1)S(1)}, bf16[8,128,384]{2,1,0:T(8,128)(2,1)S(1)}, u32[]{:S(2)}, u32[]{:S(2)}) %collective-permute-start.4) | collective-permute-done | bytes 786464 | tf_op jit(solution)/shard_map/ppermute | solution.py:495
  161.8 1.6 shard_map.70
Async XLA Ops:
  2.5 16.4 %collective-permute-start = (bf16[64,8192]{1,0:T(8,128)(2,1)}, bf16[64,8192]{1,0:T(8,128)(2,1)}, u32[]{:S(2)}, u32[]{:S(2)}) collective-permute-start(bf16[64,8192]{1,0:T(8,128)(2,1)} %get-tuple-element.11), channel_id=1, source_target_pairs={{0,2},{2,4},{4,6},{6,8},{8,10},{10,12},{12,14},{14,16},{16,18},{18... | collective-permute-start | bytes 3145736 | tf_op jit(solution)/shard_map/ppermute | solution.py:479
  4.4 14.5 %collective-permute-start.1 = (bf16[64,8192]{1,0:T(8,128)(2,1)}, bf16[64,8192]{1,0:T(8,128)(2,1)}, u32[]{:S(2)}, u32[]{:S(2)}) collective-permute-start(bf16[64,8192]{1,0:T(8,128)(2,1)} %get-tuple-element.12), channel_id=1, source_target_pairs={{0,254},{2,0},{4,2},{6,4},{8,6},{10,8},{12,10},{14,12},{16,14},{18... | collective-permute-start | bytes 3145736 | tf_op jit(solution)/shard_map/ppermute | solution.py:480
  10.1 35.6 %collective-permute-start.2 = (bf16[128,8192]{1,0:T(8,128)(2,1)}, bf16[128,8192]{1,0:T(8,128)(2,1)}, u32[]{:S(2)}, u32[]{:S(2)}) collective-permute-start(bf16[128,8192]{1,0:T(8,128)(2,1)} %get-tuple-element.13), channel_id=1, source_target_pairs={{0,254},{2,0},{4,2},{6,4},{8,6},{10,8},{12,10},{14,12},{16,14},{18... | collective-permute-start | bytes 6291464 | tf_op jit(solution)/shard_map/ppermute | solution.py:484
  10.2 35.5 %collective-permute-start.3 = (bf16[128,8192]{1,0:T(8,128)(2,1)}, bf16[128,8192]{1,0:T(8,128)(2,1)}, u32[]{:S(2)}, u32[]{:S(2)}) collective-permute-start(bf16[128,8192]{1,0:T(8,128)(2,1)} %get-tuple-element.14), channel_id=1, source_target_pairs={{0,2},{2,4},{4,6},{6,8},{8,10},{10,12},{12,14},{14,16},{16,18},{18... | collective-permute-start | bytes 6291464 | tf_op jit(solution)/shard_map/ppermute | solution.py:483
  28.3 45.3 %all-to-all-start = ((bf16[256,16,128]{2,1,0:T(8,128)(2,1)}), bf16[256,16,128]{2,1,0:T(8,128)(2,1)}, u32[]{:S(2)}, u32[]{:S(2)}) async-start(bf16[256,16,128]{2,1,0:T(8,128)(2,1)} %bitcast.8), calls=%async_computation | async-start | bytes 2097152 | tf_op jit(solution)/shard_map/all_to_all | solution.py:488
  73.5 63.0 %all-to-all-start.1 = ((bf16[256,32,128]{2,1,0:T(8,128)(2,1)}), bf16[256,32,128]{2,1,0:T(8,128)(2,1)S(1)}, u32[]{:S(2)}, u32[]{:S(2)}) async-start(bf16[256,32,128]{2,1,0:T(8,128)(2,1)} %bitcast.7), calls=%async_computation.1 | async-start | bytes 4194304 | tf_op jit(solution)/shard_map/all_to_all | solution.py:492
  140.7 21.2 %collective-permute-start.4 = (bf16[8,128,384]{2,1,0:T(8,128)(2,1)S(1)}, bf16[8,128,384]{2,1,0:T(8,128)(2,1)S(1)}, u32[]{:S(2)}, u32[]{:S(2)}) collective-permute-start(bf16[8,128,384]{2,1,0:T(8,128)(2,1)S(1)} %get-tuple-element.16), channel_id=1, source_target_pairs={{0,1},{1,0},{2,3},{3,2},{4,5},{5,4},{6,7},{7,6},{8,9},{9,8},{10,11... | collective-permute-start | bytes 2359304 | tf_op jit(solution)/shard_map/ppermute | solution.py:495
